TPU v7x, 32 devices: a whole 2x2x4 slice. The times are simulated.
32 devices in a mesh: layer: 4 (over y, core), plane: 8 (over z, x).
Axes of the slice: x: 2, y: 2, z: 4, core: 2. Of those that a mesh axis runs over, the one named last changes fastest.
Arguments:
- polar: float32 [4, 512, 512], P('layer', 'plane'), may hold values from 0.1 to 1.6
- azimuth: float32 [4, 512, 512], P('layer', 'plane'), may hold values from -3 to 3
- saturation: float32 [4, 512, 512], P('layer', 'plane'), may hold values from 0.5 to 1.5
- anisotropy: float32 [4, 512, 512], P('layer', 'plane'), may hold values from 0.3 to 1.5
- stiffness: float32 [4], P('layer'), may hold values from 0.35 to 0.7
- coupling: float32 [3], replicated, may hold values from -1 to 1
Outputs:
- field: float32 [4, 3, 512, 512], P('layer', None, 'plane')
- moment: float32 [4, 3, 512, 512], P('layer', None, 'plane')
All inputs are finite; a program needn't handle non-finite values.
Results may differ from a plain program's by a relative error of at most 0.00005.
Values sent between devices are 32-bit elements; how exact they have to be, the bound alone decides.
No kernel may reach another device: no remote copies, remote signals or barrier semaphores. Data moves between devices by JAX's collectives and lax.ppermute only.
A program may use at most 64 MiB of HBM per device.

v0:
```python
import functools
import math

import jax
import jax.numpy as jnp
import numpy as np
from jax import lax
from jax.experimental import pallas as pl
from jax.experimental.pallas import tpu as pltpu
from jax.sharding import PartitionSpec as P

side_length = 512.0
spacing = 1.2
damping = 0.1
time_step = 0.1
exact = lax.Precision.HIGHEST

lanes = 128
sublanes = 8
half = lanes // 2
root_half = math.sqrt(0.5)
chunk_count = 1
coef_count = 13
both = ("layer", "plane")
in_vmem = pl.BlockSpec(memory_space=pltpu.VMEM)
in_smem = pl.BlockSpec(memory_space=pltpu.SMEM)


def split_table(table):
    head = table.astype(np.float32).astype(jnp.bfloat16)
    rest = (table - head.astype(np.float64)).astype(np.float32).astype(jnp.bfloat16)
    return np.stack([head, rest])


def row_table(cell_count):
    turns = np.outer(np.arange(cell_count), np.arange(cell_count)) % (2 * cell_count)
    phase = turns * (np.pi / cell_count)
    return split_table(np.concatenate([np.cos(phase), -np.sin(phase)]))


def short_tables():
    turns = np.outer(np.arange(lanes), np.arange(lanes)) % lanes
    phase = turns * (2.0 * np.pi / lanes)
    c, s = np.cos(phase), np.sin(phase)
    return split_table(np.block([[c, -s], [s, c]])), split_table(np.block([[c, s], [-s, c]]))


def twiddle_table(radix):
    phase = np.outer(np.arange(radix), np.arange(lanes)) * (2.0 * np.pi / (radix * lanes))
    pair = np.stack([np.cos(phase), np.sin(phase)]).astype(np.float32)
    return np.ascontiguousarray(np.broadcast_to(pair[:, :, None], (2, radix, sublanes, lanes)))


def split(value):
    head = value.astype(jnp.bfloat16)
    return head, (value - head.astype(jnp.float32)).astype(jnp.bfloat16)


def product(left, right, dims):
    dot = functools.partial(
        lax.dot_general, dimension_numbers=(dims, ((), ())), preferred_element_type=jnp.float32
    )
    return dot(left[0], right[0]) + (dot(left[1], right[0]) + dot(left[0], right[1]))


def sine_cosine(angle):
    square = angle * angle
    sine = jnp.full_like(angle, 1.0 / math.factorial(13))
    for order in (11, 9, 7, 5, 3, 1):
        sine = (-1.0) ** ((order - 1) // 2) / math.factorial(order) + square * sine
    cosine = jnp.full_like(angle, -1.0 / math.factorial(14))
    for order in (12, 10, 8, 6, 4, 2, 0):
        cosine = (-1.0) ** (order // 2) / math.factorial(order) + square * cosine
    return angle * sine, cosine


def first_kernel(polar_ref, azimuth_ref, saturation_ref, table_ref, moment_ref, head_ref, tail_ref, *out_refs):
    rows, cell_count = polar_ref.shape
    sin_polar, cos_polar = sine_cosine(polar_ref[...])
    sin_half, cos_half = sine_cosine(0.5 * azimuth_ref[...])
    moment = (
        sin_polar * (1.0 - 2.0 * sin_half * sin_half),
        sin_polar * (2.0 * sin_half * cos_half),
        cos_polar,
    )
    for c in range(3):
        moment_ref[c] = moment[c]
        head_ref[c : c + 1] = moment[c][:1]
        tail_ref[c : c + 1] = moment[c][rows - 1 :]
    saturation = saturation_ref[...]
    magnet = [split(m * saturation) for m in moment]
    blank = jnp.zeros((rows, cell_count), jnp.bfloat16)
    for_real = [jnp.concatenate([m[n] for m in magnet] + [blank]) for n in range(2)]
    for_imag = [jnp.concatenate([blank] + [m[n] for m in magnet]) for n in range(2)]
    dims = ((1,), (1,))
    span = cell_count // len(out_refs)
    for n, out_ref in enumerate(out_refs):
        start = n * span
        cosine = (table_ref[0, start : start + span], table_ref[1, start : start + span])
        start += cell_count
        sine = (table_ref[0, start : start + span], table_ref[1, start : start + span])
        real = product(cosine, for_real, dims)
        imag = product(sine, for_imag, dims)
        out_ref[:, :lanes] = real[:, :lanes]
        out_ref[:, lanes : 2 * lanes] = real[:, lanes:] + imag[:, :lanes]
        out_ref[:, 2 * lanes :] = imag[:, lanes:]


def factors(wave_x, wave_y):
    magnitude = jnp.sqrt(wave_x * wave_x + wave_y * wave_y)
    nonzero = magnitude > 0.0
    safe = jnp.where(nonzero, magnitude, 1.0)
    inverse = 1.0 / safe
    series = jnp.ones_like(safe)
    for order in range(9, 1, -1):
        series = 1.0 - series * safe * (1.0 / order)
    growth = jnp.exp(safe)
    lost = jnp.where(safe < 0.5, series * safe, 1.0 - jnp.exp(-safe))
    self_part = jnp.where(nonzero, lost * inverse, 1.0)
    mutual = jnp.where(nonzero, lost * lost * growth * (0.5 * inverse), 0.0)
    decay = jnp.exp(-spacing * magnitude)
    unit_x = jnp.where(nonzero, wave_x * inverse, 0.0)
    unit_y = jnp.where(nonzero, wave_y * inverse, 0.0)
    return unit_x, unit_y, self_part, mutual, decay


def coef_kernel(base_ref, *out_refs, cell_count, span):
    pad_length = 2 * cell_count
    radix = pad_length // lanes
    step = math.pi / side_length
    for n, out_ref in enumerate(out_refs):
        slots = out_ref.shape[2]
        shape = (slots, lanes)
        slot = n * span + base_ref[0] * slots + lax.broadcasted_iota(jnp.int32, shape, 0)
        wave_y = step * slot.astype(jnp.float32)
        weight = jnp.where(slot == 0, 1.0, 2.0) / float(pad_length * pad_length)
        signed = jnp.where(slot % 2 == 0, weight, -weight)
        for r in range(radix):
            index = lax.broadcasted_iota(jnp.int32, shape, 1) * radix + r
            middle = index == cell_count
            folded = jnp.where(index < cell_count, index, index - pad_length)
            wave_x = step * folded.astype(jnp.float32)
            unit_x, unit_y, self_part, mutual, decay = factors(wave_x, wave_y)
            out_ref[0, r] = jnp.where(middle, 0.0, unit_x)
            out_ref[1, r] = unit_y
            out_ref[2, r] = (1.0 - self_part) * weight
            out_ref[3, r] = self_part * weight
            out_ref[4, r] = mutual * weight
            out_ref[5, r] = decay
            edge = jnp.full(shape, -step * cell_count, jnp.float32)
            edge_x, edge_y, self_part, mutual, decay = factors(wave_x, edge)
            rest = (1.0 - self_part) * signed
            mutual = mutual * signed
            square = edge_y * edge_y
            out_ref[6, r] = jnp.where(middle, 0.0, edge_x)
            out_ref[7, r] = rest
            out_ref[8, r] = self_part * signed
            out_ref[9, r] = mutual
            out_ref[10, r] = decay
            out_ref[11, r] = rest * square
            out_ref[12, r] = mutual * square


def neighbours(values, decay):
    count = len(values)
    under = [None] * count
    over = [None] * count
    for t in range(1, count):
        under[t] = decay * (values[t - 1] if under[t - 1] is None else under[t - 1] + values[t - 1])
    for t in range(count - 2, -1, -1):
        over[t] = decay * (values[t + 1] if over[t + 1] is None else over[t + 1] + values[t + 1])
    return under, over


def joined(first, second, sign=1.0):
    if first is None:
        return second if sign > 0.0 else -second
    if second is None:
        return first
    return first + second if sign > 0.0 else first - second


def drive(x, z, keep, mutual, decay, own):
    count = len(x)
    up_r, over_r = [z[t][0] + x[t][1] for t in range(count)], [x[t][1] - z[t][0] for t in range(count)]
    up_i, over_i = [z[t][1] - x[t][0] for t in range(count)], [-z[t][1] - x[t][0] for t in range(count)]
    below_r, below_i = neighbours(up_r, decay)[0], neighbours(up_i, decay)[0]
    above_r, above_i = neighbours(over_r, decay)[1], neighbours(over_i, decay)[1]
    inner, outer = [], []
    for t in range(count):
        total_r, total_i = joined(below_r[t], above_r[t]), joined(below_i[t], above_i[t])
        differ_r = joined(below_r[t], above_r[t], -1.0)
        differ_i = joined(below_i[t], above_i[t], -1.0)
        inner.append((mutual * total_i - keep * x[t][0], -(mutual * total_r) - keep * x[t][1]))
        outer.append((mutual * differ_r - own * z[t][0], mutual * differ_i - own * z[t][1]))
    return inner, outer


def even_part(values, keep, mutual, decay):
    out = []
    for n in range(2):
        part = [v[n] for v in values]
        under, over = neighbours(part, decay)
        out.append([-(keep * part[t]) - mutual * joined(under[t], over[t]) for t in range(len(part))])
    return list(zip(*out))


def respond(spectrum, coef, has_middle, middle):
    count = len(spectrum)
    unit_x, unit_y, keep, own, mutual, decay = coef[:6]
    edge_x, edge_keep, edge_own, edge_mutual, edge_decay, keep_y, mutual_y = coef[6:]
    x = [s[0] for s in spectrum]
    y = [s[1] for s in spectrum]
    z = [s[2] for s in spectrum]
    charge = [tuple(unit_x * x[t][n] + unit_y * y[t][n] for n in range(2)) for t in range(count)]
    inner, outer = drive(charge, z, keep, mutual, decay, own)
    charge = [tuple(edge_x * x[t][n] for n in range(2)) for t in range(count)]
    edge_inner, edge_outer = drive(charge, z, edge_keep, edge_mutual, edge_decay, edge_own)
    edge_y = even_part(y, keep_y, mutual_y, edge_decay)
    out = []
    for t in range(count):
        out.append(
            [
                tuple(unit_x * inner[t][n] - edge_x * edge_inner[t][n] for n in range(2)),
                tuple(unit_y * inner[t][n] - edge_y[t][n] for n in range(2)),
                tuple(outer[t][n] - edge_outer[t][n] for n in range(2)),
            ]
        )
    if has_middle:
        square = jnp.where(middle, 1.0 - unit_y * unit_y, 0.0)
        alone = even_part(x, keep * square, mutual * square, decay)
        keep_m, mutual_m = jnp.where(middle, keep_y, 0.0), jnp.where(middle, mutual_y, 0.0)
        cross_x = even_part(x, keep_m, mutual_m, edge_decay)
        cross_y = even_part(y, keep_m, mutual_m, edge_decay)
        for t in range(count):
            out[t][0] = tuple(
                out[t][0][n] + alone[t][n] - cross_x[t][n] - cross_y[t][n] for n in range(2)
            )
            out[t][1] = tuple(out[t][1][n] - cross_x[t][n] for n in range(2))
    return out


def add(a, b):
    return a[0] + b[0], a[1] + b[1]


def sub(a, b):
    return a[0] - b[0], a[1] - b[1]


def add_turned(a, b):
    return a[0] - b[1], a[1] + b[0]


def sub_turned(a, b):
    return a[0] + b[1], a[1] - b[0]


def four_point(z):
    s, d, u, v = add(z[0], z[2]), sub(z[0], z[2]), add(z[1], z[3]), sub(z[1], z[3])
    return add(s, u), sub_turned(d, v), sub(s, u), add_turned(d, v)


def four_point_back(z):
    s, d, u, v = add(z[0], z[2]), sub(z[0], z[2]), add(z[1], z[3]), sub(z[1], z[3])
    return add(s, u), add_turned(d, v), sub(s, u), sub_turned(d, v)


def spread(z):
    turned = [
        z[0],
        (root_half * (z[1][0] + z[1][1]), root_half * (z[1][1] - z[1][0])),
        (z[2][1], -z[2][0]),
        (root_half * (z[3][1] - z[3][0]), -root_half * (z[3][0] + z[3][1])),
    ]
    even, odd = four_point(z), four_point(turned)
    return [even[r // 2] if r % 2 == 0 else odd[r // 2] for r in range(8)]


def gather_back(v):
    even, odd = four_point_back(v[0::2]), four_point_back(v[1::2])
    return [
        add(even[0], odd[0]),
        (even[1][0] + root_half * (odd[1][0] - odd[1][1]), even[1][1] + root_half * (odd[1][0] + odd[1][1])),
        add_turned(even[2], odd[2]),
        (even[3][0] - root_half * (odd[3][0] + odd[3][1]), even[3][1] + root_half * (odd[3][0] - odd[3][1])),
    ]


def middle_kernel(rows_ref, coef_ref, twiddle_ref, forward_ref, back_ref, out_ref, work_ref, *, layers):
    radix = twiddle_ref.shape[1]
    pieces = radix // 2
    planes = rows_ref.shape[0] // layers
    items = layers * 3
    place = lax.broadcasted_iota(jnp.int32, (sublanes, lanes), 1)
    low = place < half

    def piece(row, part):
        tile, upper = divmod(part, 2)
        cut = slice(tile * lanes, (tile + 1) * lanes)
        first, second = rows_ref[row, :, cut], rows_ref[row + 1, :, cut]
        if upper:
            return jnp.where(low, pltpu.roll(first, half, 1), second)
        return jnp.where(low, first, pltpu.roll(second, half, 1))

    for item in range(items):
        layer, c = divmod(item, 3)
        z = [
            (piece(layer * planes + 2 * p, c), piece(layer * planes + 2 * p, 3 + c)) for p in range(pieces)
        ]
        for r, (real, imag) in enumerate(spread(z)):
            if r > 0:
                cosine, sine = twiddle_ref[0, r], twiddle_ref[1, r]
                real, imag = real * cosine + imag * sine, imag * cosine - real * sine
            start = item * sublanes
            work_ref[r, start : start + sublanes, :lanes] = real
            work_ref[r, start : start + sublanes, lanes:] = imag
    dims = ((1,), (0,))
    forward = (forward_ref[0], forward_ref[1])
    back = (back_ref[0], back_ref[1])
    for r in range(radix):
        value = product(split(work_ref[r]), forward, dims)
        spectrum = [
            [
                (
                    value[(t * 3 + c) * sublanes : (t * 3 + c + 1) * sublanes, :lanes],
                    value[(t * 3 + c) * sublanes : (t * 3 + c + 1) * sublanes, lanes:],
                )
                for c in range(3)
            ]
            for t in range(layers)
        ]
        coef = [coef_ref[n, r] for n in range(coef_count)]
        out = respond(spectrum, coef, r == 0, place * radix + r == radix * half)
        value = jnp.concatenate(
            [jnp.concatenate([pair[0], pair[1]], axis=1) for layer in out for pair in layer]
        )
        work_ref[r] = product(split(value), back, dims)
    for layer in range(layers):
        parts = [[None] * 6 for _ in range(pieces)]
        for c in range(3):
            start = (layer * 3 + c) * sublanes
            v = []
            for r in range(radix):
                real = work_ref[r, start : start + sublanes, :lanes]
                imag = work_ref[r, start : start + sublanes, lanes:]
                if r > 0:
                    cosine, sine = twiddle_ref[0, r], twiddle_ref[1, r]
                    real, imag = real * cosine - imag * sine, imag * cosine + real * sine
                v.append((real, imag))
            for p, (real, imag) in enumerate(gather_back(v)):
                parts[p][c], parts[p][3 + c] = real, imag
        for p in range(pieces):
            row = layer * planes + 2 * p
            for tile in range(3):
                first, second = parts[p][2 * tile], parts[p][2 * tile + 1]
                cut = slice(tile * lanes, (tile + 1) * lanes)
                out_ref[row, :, cut] = jnp.where(low, first, pltpu.roll(second, half, 1))
                out_ref[row + 1, :, cut] = jnp.where(low, pltpu.roll(first, half, 1), second)


def exchange_kernel(link_ref, moment_ref, below_ref, above_ref, before_ref, after_ref, anisotropy_ref, out_ref):
    rows, cell_count = anisotropy_ref.shape
    row = lax.broadcasted_iota(jnp.int32, (rows, cell_count), 0)
    column = lax.broadcasted_iota(jnp.int32, (rows, cell_count), 1)
    stiffness, lower_link, upper_link = link_ref[0], link_ref[1], link_ref[2]
    for c in range(3):
        m = moment_ref[c]
        before = jnp.where(row == 0, before_ref[c : c + 1], pltpu.roll(m, 1, 0))
        after = jnp.where(row == rows - 1, after_ref[c : c + 1], pltpu.roll(m, rows - 1, 0))
        left = jnp.where(column == 0, 0.0, pltpu.roll(m, 1, 1))
        right = jnp.where(column == cell_count - 1, 0.0, pltpu.roll(m, cell_count - 1, 1))
        total = stiffness * (before + after + left + right)
        total = total + lower_link * below_ref[c] + upper_link * above_ref[c]
        if c == 2:
            total = total + anisotropy_ref[...] * m
        out_ref[c] = total


def inverse_rows(block_refs, table_ref, cell_count, rows):
    span = cell_count // len(block_refs)
    dims = ((1,), (0,))
    total = None
    for n, block_ref in enumerate(block_refs):
        turned = block_ref[...].T
        for part in range(2):
            start = part * cell_count + n * span
            table = (table_ref[0, start : start + span], table_ref[1, start : start + span])
            term = product(split(turned[part * 3 * rows : (part + 1) * 3 * rows]), table, dims)
            total = term if total is None else total + term
    return total


def last_kernel(moment_ref, other_ref, table_ref, *refs):
    block_refs, (field_ref, out_ref) = refs[:-2], refs[-2:]
    rows, cell_count = moment_ref.shape[1:]
    demag = inverse_rows(block_refs, table_ref, cell_count, rows)
    m = [moment_ref[c] for c in range(3)]
    f = [other_ref[c] + demag[c * rows : (c + 1) * rows] for c in range(3)]
    first = cross(m, f)
    second = cross(m, first)
    stepped = []
    for c in range(3):
        field_ref[c] = f[c]
        torque = -(first[c] + damping * second[c]) / (1.0 + damping * damping)
        stepped.append(m[c] + time_step * torque)
    scale = lax.rsqrt(stepped[0] * stepped[0] + stepped[1] * stepped[1] + stepped[2] * stepped[2])
    for c in range(3):
        out_ref[c] = stepped[c] * scale


def cross(first, second):
    return [
        first[1] * second[2] - first[2] * second[1],
        first[2] * second[0] - first[0] * second[2],
        first[0] * second[1] - first[1] * second[0],
    ]


def shift(value, axis, step):
    count = lax.axis_size(axis)
    pairs = [(i, i + step) for i in range(count) if 0 <= i + step < count]
    return lax.ppermute(value, axis, pairs)


def fast_body(polar, azimuth, saturation, anisotropy, stiffness, coupling):
    rows, cell_count = polar.shape[1:]
    layers, planes = lax.axis_size("layer"), lax.axis_size("plane")
    device_count = layers * planes
    layer_index = lax.axis_index("layer")
    plane_index = lax.axis_index("plane")
    span = cell_count // chunk_count
    slots = span // device_count
    radix = 2 * cell_count // lanes
    width = 6 * rows
    f32 = jnp.float32
    table = jnp.asarray(row_table(cell_count))
    forward, back = (jnp.asarray(t) for t in short_tables())
    twiddle = jnp.asarray(twiddle_table(radix))

    moment, top, bottom, *sent = pl.pallas_call(
        first_kernel,
        out_shape=[
            jax.ShapeDtypeStruct((3, rows, cell_count), f32),
            jax.ShapeDtypeStruct((sublanes, cell_count), f32),
            jax.ShapeDtypeStruct((sublanes, cell_count), f32),
        ]
        + [jax.ShapeDtypeStruct((span, width), f32)] * chunk_count,
        in_specs=[in_vmem] * 4,
        out_specs=[in_vmem] * (3 + chunk_count),
        cost_estimate=pl.CostEstimate(
            flops=12 * rows * cell_count * cell_count * 6, bytes_accessed=8 << 20, transcendentals=0
        ),
        name="first",
    )(polar[0], azimuth[0], saturation[0], table)

    base = (layer_index * planes + plane_index).astype(jnp.int32).reshape(1)
    coefs = pl.pallas_call(
        functools.partial(coef_kernel, cell_count=cell_count, span=span),
        out_shape=[jax.ShapeDtypeStruct((coef_count, radix, slots, lanes), f32)] * chunk_count,
        in_specs=[in_smem],
        out_specs=[in_vmem] * chunk_count,
        cost_estimate=pl.CostEstimate(flops=20 << 20, bytes_accessed=1 << 20, transcendentals=1 << 16),
        name="coefs",
    )(base)

    below = shift(moment, "layer", 1)
    above = shift(moment, "layer", -1)
    before = shift(bottom, "plane", 1)
    after = shift(top, "plane", -1)
    links = jnp.stack(
        [
            stiffness[0],
            coupling[jnp.maximum(layer_index - 1, 0)],
            coupling[jnp.minimum(layer_index, coupling.shape[0] - 1)],
        ]
    )
    other = pl.pallas_call(
        exchange_kernel,
        out_shape=jax.ShapeDtypeStruct((3, rows, cell_count), f32),
        in_specs=[in_smem] + [in_vmem] * 6,
        out_specs=in_vmem,
        cost_estimate=pl.CostEstimate(flops=20 << 20, bytes_accessed=2 << 20, transcendentals=0),
        name="exchange",
    )(links, moment, below, above, before, after, anisotropy[0])

    received = []
    for n in range(chunk_count):
        block = sent[n].reshape(device_count, slots, width)
        block = lax.all_to_all(block, both, split_axis=0, concat_axis=0, tiled=True)
        block = pl.pallas_call(
            functools.partial(middle_kernel, layers=layers),
            grid=(slots // sublanes,),
            out_shape=jax.ShapeDtypeStruct((device_count, slots, width), f32),
            in_specs=[
                pl.BlockSpec((device_count, sublanes, width), lambda g: (0, g, 0)),
                pl.BlockSpec((coef_count, radix, sublanes, lanes), lambda g: (0, 0, g, 0)),
                pl.BlockSpec((2, radix, sublanes, lanes), lambda g: (0, 0, 0, 0)),
                pl.BlockSpec((2, 2 * lanes, 2 * lanes), lambda g: (0, 0, 0)),
                pl.BlockSpec((2, 2 * lanes, 2 * lanes), lambda g: (0, 0, 0)),
            ],
            out_specs=pl.BlockSpec((device_count, sublanes, width), lambda g: (0, g, 0)),
            scratch_shapes=[pltpu.VMEM((radix, layers * 3 * sublanes, 2 * lanes), f32)],
            cost_estimate=pl.CostEstimate(flops=2000 << 20, bytes_accessed=4 << 20, transcendentals=0),
            name="middle",
        )(block, coefs[n], twiddle, forward, back)
        block = lax.all_to_all(block, both, split_axis=0, concat_axis=0, tiled=True)
        received.append(block.reshape(span, width))

    field, stepped = pl.pallas_call(
        last_kernel,
        out_shape=[jax.ShapeDtypeStruct((3, rows, cell_count), f32)] * 2,
        in_specs=[in_vmem] * (3 + chunk_count),
        out_specs=[in_vmem] * 2,
        cost_estimate=pl.CostEstimate(
            flops=12 * rows * cell_count * cell_count * 6, bytes_accessed=8 << 20, transcendentals=0
        ),
        name="last",
    )(moment, other, table, *received)
    return field[None], stepped[None]


def with_halo(cells, sides, width):
    for axis, dim in sides:
        count = lax.axis_size(axis)
        ends = count - 1
        head = lax.slice_in_dim(cells, 0, width, axis=dim)
        tail = lax.slice_in_dim(cells, cells.shape[dim] - width, cells.shape[dim], axis=dim)
        cells = jnp.concatenate(
            [
                lax.ppermute(tail, axis, [(i, (i + 1) % count) for i in range(ends)]),
                cells,
                lax.ppermute(head, axis, [((i + 1) % count, i) for i in range(ends)]),
            ],
            axis=dim,
        )
    return cells


def cross_product(first, second):
    return jnp.stack(
        [
            first[1] * second[2] - first[2] * second[1],
            first[2] * second[0] - first[0] * second[2],
            first[0] * second[1] - first[1] * second[0],
        ]
    )


def signed_wave(index, cell_count):
    folded = jnp.where(index < cell_count, index, index - 2 * cell_count)
    return jnp.pi * folded.astype(jnp.float32) / side_length


def plain_body(polar, azimuth, saturation, anisotropy, stiffness, coupling):
    row_count = polar.shape[1]
    cell_count = polar.shape[2]
    pad_length = 2 * cell_count
    plane_count = lax.axis_size("plane")
    band_width = pad_length // plane_count
    layer_index = lax.axis_index("layer")
    plane_index = lax.axis_index("plane")
    theta = polar[0]
    azimuthal = azimuth[0]
    moment_in = jnp.stack(
        [jnp.sin(theta) * jnp.cos(azimuthal), jnp.sin(theta) * jnp.sin(azimuthal), jnp.cos(theta)]
    )
    magnet = moment_in * saturation[0][None]
    place = jnp.arange(cell_count, dtype=jnp.int32)
    wave_index = jnp.arange(pad_length, dtype=jnp.int32)
    turns = place[:, None] * wave_index[None, :] % pad_length
    phase = turns.astype(jnp.float32) * (2.0 * jnp.pi / pad_length)
    cosine = jnp.cos(phase)
    sine = jnp.sin(phase)
    cosine_blocks = cosine.reshape(plane_count, row_count, pad_length)
    sine_blocks = sine.reshape(plane_count, row_count, pad_length)
    cosine_bands = cosine.reshape(cell_count, plane_count, band_width)
    sine_bands = sine.reshape(cell_count, plane_count, band_width)
    along_real = jnp.einsum("cxy,yk->ckx", magnet, cosine, precision=exact)
    along_imag = -jnp.einsum("cxy,yk->ckx", magnet, sine, precision=exact)
    sectioned = jnp.stack([along_real, along_imag], 1).reshape(
        3, 2, plane_count, band_width * row_count
    )
    block = lax.all_to_all(sectioned, "plane", split_axis=2, concat_axis=2, tiled=True)
    item_count = block.shape[0]
    split = block.reshape(item_count, 2, plane_count, band_width, row_count)
    with_cosine = jnp.einsum("npsqx,sxk->npqk", split, cosine_blocks, precision=exact)
    with_sine = jnp.einsum("npsqx,sxk->npqk", split, sine_blocks, precision=exact)
    spectrum = jnp.stack(
        [with_cosine[:, 0] + with_sine[:, 1], with_cosine[:, 1] - with_sine[:, 0]], 1
    )
    wave_y = signed_wave(
        plane_index * band_width + jnp.arange(band_width, dtype=jnp.int32), cell_count
    )[:, None]
    wave_x = signed_wave(wave_index, cell_count)[None, :]
    magnitude = jnp.sqrt(wave_x * wave_x + wave_y * wave_y)
    nonzero = magnitude > 0.0
    safe = jnp.where(nonzero, magnitude, 1.0)
    unit_x = jnp.where(nonzero, wave_x / safe, 0.0)
    unit_y = jnp.where(nonzero, wave_y / safe, 0.0)
    self_part = jnp.where(nonzero, -jnp.expm1(-safe) / safe, 1.0)
    half_sinh = jnp.sinh(0.5 * safe)
    mutual = jnp.where(nonzero, 2.0 * half_sinh * half_sinh / safe, 0.0)
    spectral_x = spectrum[0]
    spectral_y = spectrum[1]
    spectral_z = spectrum[2]
    inplane = unit_x * spectral_x + unit_y * spectral_y
    upward = jnp.stack([spectral_z[0] + inplane[1], spectral_z[1] - inplane[0]])
    downward = jnp.stack([-spectral_z[0] + inplane[1], -spectral_z[1] - inplane[0]])
    emitted = jnp.stack([upward, downward])[None]
    piece = lax.all_gather(emitted, "layer", axis=0, tiled=True)
    source = jnp.arange(piece.shape[0], dtype=jnp.int32)
    separation = layer_index - source
    distance = jnp.abs(separation).astype(jnp.float32)
    weight = jnp.exp(-spacing * distance[:, None, None] * magnitude[None])
    lower = jnp.where((separation > 0)[:, None, None], weight, 0.0)
    upper = jnp.where((separation < 0)[:, None, None], weight, 0.0)
    below = jnp.sum(lower[:, None] * piece[:, 0], 0)
    above = jnp.sum(upper[:, None] * piece[:, 1], 0)
    total = below + above
    differ = below - above
    remainder = 1.0 - self_part
    field_x = jnp.stack(
        [
            -remainder * unit_x * inplane[0] + unit_x * mutual * total[1],
            -remainder * unit_x * inplane[1] - unit_x * mutual * total[0],
        ]
    )
    field_y = jnp.stack(
        [
            -remainder * unit_y * inplane[0] + unit_y * mutual * total[1],
            -remainder * unit_y * inplane[1] - unit_y * mutual * total[0],
        ]
    )
    field_z = jnp.stack(
        [
            -self_part * spectral_z[0] + mutual * differ[0],
            -self_part * spectral_z[1] + mutual * differ[1],
        ]
    )
    spectral = jnp.stack([field_x, field_y, field_z])
    back_cosine = jnp.einsum("cpqk,sxk->cpsqx", spectral, cosine_blocks, precision=exact)
    back_sine = jnp.einsum("cpqk,sxk->cpsqx", spectral, sine_blocks, precision=exact)
    returned = jnp.stack(
        [back_cosine[:, 0] - back_sine[:, 1], back_sine[:, 0] + back_cosine[:, 1]], 1
    )
    returned = returned.reshape(3, 2, plane_count, band_width * row_count)
    scale = 1.0 / (float(pad_length) * float(pad_length))
    block = lax.all_to_all(returned, "plane", split_axis=2, concat_axis=2, tiled=True)
    item_count = block.shape[0]
    split = block.reshape(item_count, 2, plane_count, band_width, row_count)
    real_part = jnp.einsum("nsqx,ysq->nxy", split[:, 0], cosine_bands, precision=exact)
    imag_part = jnp.einsum("nsqx,ysq->nxy", split[:, 1], sine_bands, precision=exact)
    demag = (real_part - imag_part) * scale
    padded = with_halo(moment_in[None], (("layer", 0), ("plane", 2)), 1)
    centre = padded[1]
    beside = centre[:, :-2] + centre[:, 2:]
    sideways = jnp.pad(moment_in, ((0, 0), (0, 0), (1, 1)))
    beside = beside + sideways[:, :, :-2] + sideways[:, :, 2:]
    lower_link = coupling[jnp.maximum(layer_index - 1, 0)]
    upper_link = coupling[jnp.minimum(layer_index, coupling.shape[0] - 1)]
    exchange_field = (
        stiffness[0] * beside + lower_link * padded[0, :, 1:-1] + upper_link * padded[2, :, 1:-1]
    )
    flat_zero = jnp.zeros_like(moment_in[2])
    uniaxial = jnp.stack([flat_zero, flat_zero, anisotropy[0] * moment_in[2]])
    field = demag + exchange_field + uniaxial
    first_cross = cross_product(moment_in, field)
    second_cross = cross_product(moment_in, first_cross)
    torque = -(first_cross + damping * second_cross) / (1.0 + damping * damping)
    stepped = moment_in + time_step * torque
    length = jnp.sqrt(jnp.sum(stepped * stepped, axis=0, keepdims=True))
    return (field[None], (stepped / length)[None])


def body(polar, azimuth, saturation, anisotropy, stiffness, coupling):
    rows, cell_count = polar.shape[1:]
    device_count = lax.axis_size("layer") * lax.axis_size("plane")
    fits = 2 * rows == lanes and cell_count == 4 * lanes
    fits = fits and cell_count % (chunk_count * device_count * sublanes) == 0
    chosen = fast_body if fits else plain_body
    return chosen(polar, azimuth, saturation, anisotropy, stiffness, coupling)


def solution(mesh):
    placed = (
        P("layer", "plane", None),
        P("layer", "plane", None),
        P("layer", "plane", None),
        P("layer", "plane", None),
        P("layer"),
        P(),
    )
    return jax.shard_map(
        body,
        mesh=mesh,
        in_specs=placed,
        out_specs=(P("layer", None, "plane", None), P("layer", None, "plane", None)),
        check_vma=False,
    )
```

profile of v0, /device:TPU:0, one launch (start us, length us, event | category | flops | bytes accessed | tf_op | source)
XLA Modules:
  0.0 69.2 jit_solution(6706144463085423559)
XLA Ops:
  0.6 3.9 %first.1 = (f32[3,64,512]{2,1,0:T(8,128)}, f32[8,512]{1,0:T(8,128)}, f32[8,512]{1,0:T(8,128)}, f32[512,384]{1,0:T(8,128)}) custom-call(f32[64,512]{1,0:T(8,128)} %bitcast.12, f32[64,512]{1,0:T(8,128)} %bitcast.13, f32[64,512]{1,0:T(8,128)} %bitcast.14, bf16[2,1024,512]{2,1,0:T(8,128)(2,1)} %constant.28.clone.table_ref), custom_call_target="tpu_custom_call" | custom-call | flops 1207959552 | bytes 8388608 | tf_op jit(solution)/shard_map/first/pallas_call | solution.py:441
  4.5 7.3 %all-to-all-start = ((f32[32,16,384]{2,1,0:T(8,128)}), f32[32,16,384]{2,1,0:T(8,128)S(1)}, u32[]{:S(2)}, u32[]{:S(2)}) async-start(f32[32,16,384]{2,1,0:T(8,128)} %bitcast.10), calls=%async_computation | async-start | bytes 1572864 | tf_op jit(solution)/shard_map/all_to_all | solution.py:490
  11.9 1.1 %coefs.1.coef_ref = f32[13,8,16,128]{3,2,1,0:T(8,128)} custom-call(s32[1]{0:T(128)} %bitcast.5.base_ref), custom_call_target="tpu_custom_call" | custom-call | flops 20971520 | bytes 1048576 | tf_op jit(solution)/shard_map/coefs/pallas_call | solution.py:458
  13.0 0.0 copy-start.2
  13.0 0.0 copy-start.9
  13.1 20.7 %all-to-all-done.rows_ref = f32[32,16,384]{2,1,0:T(8,128)S(1)} async-done(((f32[32,16,384]{2,1,0:T(8,128)}), f32[32,16,384]{2,1,0:T(8,128)S(1)}, u32[]{:S(2)}, u32[]{:S(2)}) %all-to-all-start) | async-done | bytes 786464 | tf_op jit(solution)/shard_map/all_to_all | solution.py:490
  33.7 0.9 %copy-done.1 = f32[32,16,384]{2,1,0:T(8,128)} copy-done((f32[32,16,384]{2,1,0:T(8,128)}, f32[32,16,384]{2,1,0:T(8,128)S(1)}, u32[]{:S(2)}) %copy-start.1) | copy-done | bytes 786456
  34.6 5.3 %middle.1 = f32[32,16,384]{2,1,0:T(8,128)} custom-call(f32[32,16,384]{2,1,0:T(8,128)} %copy-done.1, f32[13,8,16,128]{3,2,1,0:T(8,128)} %coefs.1.coef_ref, f32[2,8,8,128]{3,2,1,0:T(8,128)} %constant.31.clone.twiddle_ref, bf16[2,256,256]{2,1,0:T(8,128)(2,1)} %constant.29.clone.forward_ref, bf16[2,256,256]{2,1,0:T(8,128)(2,1)} %constant.30.clone.back_ref), custom_call_target="tpu_custom_call" | custom-call | flops 2097152000 | bytes 4194304 | tf_op jit(solution)/shard_map/middle/pallas_call | solution.py:491
  39.9 2.6 %all-to-all-start.1 = ((f32[32,16,384]{2,1,0:T(8,128)}), f32[32,16,384]{2,1,0:T(8,128)S(1)}, u32[]{:S(2)}, u32[]{:S(2)}) async-start(f32[32,16,384]{2,1,0:T(8,128)} %middle.1), calls=%async_computation.1 | async-start | bytes 1572864 | tf_op jit(solution)/shard_map/all_to_all | solution.py:507
  42.6 0.0 copy-done.2
  42.6 1.3 %collective-permute-start.1 = (f32[3,64,512]{2,1,0:T(8,128)S(1)}, f32[3,64,512]{2,1,0:T(8,128)S(1)}, u32[]{:S(2)}, u32[]{:S(2)}) collective-permute-start(f32[3,64,512]{2,1,0:T(8,128)S(1)} %copy-done.2), channel_id=1, source_target_pairs={{8,0},{16,8},{24,16},{9,1},{17,9},{25,17},{10,2},{18,10},{26,18},{... | collective-permute-start | bytes 1179656 | tf_op jit(solution)/shard_map/ppermute | solution.py:423
  43.9 3.1 %collective-permute-start = (f32[3,64,512]{2,1,0:T(8,128)S(1)}, f32[3,64,512]{2,1,0:T(8,128)S(1)}, u32[]{:S(2)}, u32[]{:S(2)}) collective-permute-start(f32[3,64,512]{2,1,0:T(8,128)S(1)} %copy-done.2), channel_id=1, source_target_pairs={{0,8},{8,16},{16,24},{1,9},{9,17},{17,25},{2,10},{10,18},{18,26},{... | collective-permute-start | bytes 1179656 | tf_op jit(solution)/shard_map/ppermute | solution.py:423
  47.0 0.0 copy-done.9
  47.0 3.5 %collective-permute-start.2 = (f32[8,512]{1,0:T(8,128)S(1)}, f32[8,512]{1,0:T(8,128)S(1)}, u32[]{:S(2)}, u32[]{:S(2)}) collective-permute-start(f32[8,512]{1,0:T(8,128)S(1)} %copy-done.9), channel_id=1, source_target_pairs={{0,1},{1,2},{2,3},{3,4},{4,5},{5,6},{6,7},{8,9},{9,10},{10,11},{11... | collective-permute-start | bytes 49160 | tf_op jit(solution)/shard_map/ppermute | solution.py:423
  50.5 0.0 copy-done.8
  50.5 1.3 %collective-permute-start.3 = (f32[8,512]{1,0:T(8,128)S(1)}, f32[8,512]{1,0:T(8,128)S(1)}, u32[]{:S(2)}, u32[]{:S(2)}) collective-permute-start(f32[8,512]{1,0:T(8,128)S(1)} %copy-done.8), channel_id=1, source_target_pairs={{1,0},{2,1},{3,2},{4,3},{5,4},{6,5},{7,6},{9,8},{10,9},{11,10},{12... | collective-permute-start | bytes 49160 | tf_op jit(solution)/shard_map/ppermute | solution.py:423
  52.5 0.0 copy-done.7
  52.5 0.6 fusion
  53.1 1.9 %pad_maximum_fusion.link_ref = f32[3]{0:T(128)} fusion(f32[1]{0:T(128)} %get-tuple-element.15, f32[1]{0:T(128)} %get-tuple-element.14, f32[1]{0:T(128)S(6)} %copy.12), kind=kLoop, calls=%fused_computation | loop fusion | flops 6 | bytes 24 | tf_op jit(solution)/shard_map/stack | solution.py:471
  55.0 0.0 collective-permute-done.2.before_ref
  55.0 1.4 %collective-permute-done.3.after_ref = f32[8,512]{1,0:T(8,128)S(1)} collective-permute-done((f32[8,512]{1,0:T(8,128)S(1)}, f32[8,512]{1,0:T(8,128)S(1)}, u32[]{:S(2)}, u32[]{:S(2)}) %collective-permute-start.3) | collective-permute-done | bytes 16416 | tf_op jit(solution)/shard_map/ppermute | solution.py:423
  56.4 0.0 collective-permute-done.1.above_ref
  56.4 0.0 collective-permute-done.below_ref
  56.4 0.0 copy-start.4
  56.4 0.0 copy-done.5
  56.4 0.6 copy-done.6
  57.0 0.2 copy-done.3
  57.1 0.1 copy-done.4
  57.2 2.4 %exchange.1.other_ref = f32[3,64,512]{2,1,0:T(8,128)} custom-call(f32[3]{0:T(128)} %pad_maximum_fusion.link_ref, f32[3,64,512]{2,1,0:T(8,128)} %get-tuple-element.8.moment_ref, f32[3,64,512]{2,1,0:T(8,128)} %copy-done.4, f32[3,64,512]{2,1,0:T(8,128)} %copy-done.3, f32[8,512]{1,0:T(8,128)} %copy-done.5, f32[8,512]{1,0:T(8,128)} %copy-done.6, f32[64,512]{1,0:T(8,128)} %bitcast.11), custom_call_target="tpu_custom_call" | custom-call | flops 20971520 | bytes 2097152 | tf_op jit(solution)/shard_map/exchange/pallas_call | solution.py:478
  59.7 4.8 %all-to-all-done.1 = f32[32,16,384]{2,1,0:T(8,128)S(1)} async-done(((f32[32,16,384]{2,1,0:T(8,128)}), f32[32,16,384]{2,1,0:T(8,128)S(1)}, u32[]{:S(2)}, u32[]{:S(2)}) %all-to-all-start.1) | async-done | bytes 786464 | tf_op jit(solution)/shard_map/all_to_all | solution.py:507
  64.4 0.9 %copy-done = f32[32,16,384]{2,1,0:T(8,128)} copy-done((f32[32,16,384]{2,1,0:T(8,128)}, f32[32,16,384]{2,1,0:T(8,128)S(1)}, u32[]{:S(2)}) %copy-start) | copy-done | bytes 786456
  65.3 3.9 %last.1 = (f32[3,64,512]{2,1,0:T(8,128)}, f32[3,64,512]{2,1,0:T(8,128)}) custom-call(f32[3,64,512]{2,1,0:T(8,128)} %get-tuple-element.8.moment_ref, f32[3,64,512]{2,1,0:T(8,128)} %exchange.1.other_ref, bf16[2,1024,512]{2,1,0:T(8,128)(2,1)} %constant.28.clone.table_ref, f32[512,384]{1,0:T(8,128)} %bitcast.9), custom_call_target="tpu_custom_call" | custom-call | flops 1207959552 | bytes 8388608 | tf_op jit(solution)/shard_map/last/pallas_call | solution.py:510
  (7 shorter events, 0.0 us)
Async XLA Ops:
  4.5 29.2 %all-to-all-start = ((f32[32,16,384]{2,1,0:T(8,128)}), f32[32,16,384]{2,1,0:T(8,128)S(1)}, u32[]{:S(2)}, u32[]{:S(2)}) async-start(f32[32,16,384]{2,1,0:T(8,128)} %bitcast.10), calls=%async_computation | async-start | bytes 1572864 | tf_op jit(solution)/shard_map/all_to_all | solution.py:490
  13.0 29.5 %copy-start.2 = (f32[3,64,512]{2,1,0:T(8,128)S(1)}, f32[3,64,512]{2,1,0:T(8,128)}, u32[]{:S(2)}) copy-start(f32[3,64,512]{2,1,0:T(8,128)} %get-tuple-element.8.moment_ref) | copy-start | bytes 1179652
  13.0 33.9 %copy-start.9 = (f32[8,512]{1,0:T(8,128)S(1)}, f32[8,512]{1,0:T(8,128)}, u32[]{:S(2)}) copy-start(f32[8,512]{1,0:T(8,128)} %get-tuple-element.9) | copy-start | bytes 49156
  13.0 37.5 %copy-start.8 = (f32[8,512]{1,0:T(8,128)S(1)}, f32[8,512]{1,0:T(8,128)}, u32[]{:S(2)}) copy-start(f32[8,512]{1,0:T(8,128)} %get-tuple-element.10) | copy-start | bytes 49156
  13.0 39.4 %copy-start.7 = (f32[3]{0:T(128)S(1)}, f32[3]{0:T(128)}, u32[]{:S(2)}) copy-start(f32[3]{0:T(128)} %param.15) | copy-start | bytes 40
  33.7 0.9 %copy-start.1 = (f32[32,16,384]{2,1,0:T(8,128)}, f32[32,16,384]{2,1,0:T(8,128)S(1)}, u32[]{:S(2)}) copy-start(f32[32,16,384]{2,1,0:T(8,128)S(1)} %all-to-all-done.rows_ref) | copy-start | bytes 2359300
  39.9 24.5 %all-to-all-start.1 = ((f32[32,16,384]{2,1,0:T(8,128)}), f32[32,16,384]{2,1,0:T(8,128)S(1)}, u32[]{:S(2)}, u32[]{:S(2)}) async-start(f32[32,16,384]{2,1,0:T(8,128)} %middle.1), calls=%async_computation.1 | async-start | bytes 1572864 | tf_op jit(solution)/shard_map/all_to_all | solution.py:507
  42.6 13.8 %collective-permute-start.1 = (f32[3,64,512]{2,1,0:T(8,128)S(1)}, f32[3,64,512]{2,1,0:T(8,128)S(1)}, u32[]{:S(2)}, u32[]{:S(2)}) collective-permute-start(f32[3,64,512]{2,1,0:T(8,128)S(1)} %copy-done.2), channel_id=1, source_target_pairs={{8,0},{16,8},{24,16},{9,1},{17,9},{25,17},{10,2},{18,10},{26,18},{... | collective-permute-start | bytes 1179656 | tf_op jit(solution)/shard_map/ppermute | solution.py:423
  43.9 12.5 %collective-permute-start = (f32[3,64,512]{2,1,0:T(8,128)S(1)}, f32[3,64,512]{2,1,0:T(8,128)S(1)}, u32[]{:S(2)}, u32[]{:S(2)}) collective-permute-start(f32[3,64,512]{2,1,0:T(8,128)S(1)} %copy-done.2), channel_id=1, source_target_pairs={{0,8},{8,16},{16,24},{1,9},{9,17},{17,25},{2,10},{10,18},{18,26},{... | collective-permute-start | bytes 1179656 | tf_op jit(solution)/shard_map/ppermute | solution.py:423
  47.0 8.0 %collective-permute-start.2 = (f32[8,512]{1,0:T(8,128)S(1)}, f32[8,512]{1,0:T(8,128)S(1)}, u32[]{:S(2)}, u32[]{:S(2)}) collective-permute-start(f32[8,512]{1,0:T(8,128)S(1)} %copy-done.9), channel_id=1, source_target_pairs={{0,1},{1,2},{2,3},{3,4},{4,5},{5,6},{6,7},{8,9},{9,10},{10,11},{11... | collective-permute-start | bytes 49160 | tf_op jit(solution)/shard_map/ppermute | solution.py:423
  50.5 5.8 %collective-permute-start.3 = (f32[8,512]{1,0:T(8,128)S(1)}, f32[8,512]{1,0:T(8,128)S(1)}, u32[]{:S(2)}, u32[]{:S(2)}) collective-permute-start(f32[8,512]{1,0:T(8,128)S(1)} %copy-done.8), channel_id=1, source_target_pairs={{1,0},{2,1},{3,2},{4,3},{5,4},{6,5},{7,6},{9,8},{10,9},{11,10},{12... | collective-permute-start | bytes 49160 | tf_op jit(solution)/shard_map/ppermute | solution.py:423
  55.0 1.4 %copy-start.5 = (f32[8,512]{1,0:T(8,128)}, f32[8,512]{1,0:T(8,128)S(1)}, u32[]{:S(2)}) copy-start(f32[8,512]{1,0:T(8,128)S(1)} %collective-permute-done.2.before_ref) | copy-start | bytes 49156
  56.4 0.6 copy-start.6
  56.4 0.7 %copy-start.3 = (f32[3,64,512]{2,1,0:T(8,128)}, f32[3,64,512]{2,1,0:T(8,128)S(1)}, u32[]{:S(2)}) copy-start(f32[3,64,512]{2,1,0:T(8,128)S(1)} %collective-permute-done.1.above_ref) | copy-start | bytes 1179652
  56.4 0.9 %copy-start.4 = (f32[3,64,512]{2,1,0:T(8,128)}, f32[3,64,512]{2,1,0:T(8,128)S(1)}, u32[]{:S(2)}) copy-start(f32[3,64,512]{2,1,0:T(8,128)S(1)} %collective-permute-done.below_ref) | copy-start | bytes 1179652
  64.4 0.9 %copy-start = (f32[32,16,384]{2,1,0:T(8,128)}, f32[32,16,384]{2,1,0:T(8,128)S(1)}, u32[]{:S(2)}) copy-start(f32[32,16,384]{2,1,0:T(8,128)S(1)} %all-to-all-done.1) | copy-start | bytes 2359300
where the time goes:
time: 69.7 us; the launch traced here: 69.2 us
  waiting for transfers between devices  26.9 us (39%)
  starting transfers between devices  19.1 us (27%)
  Pallas kernels  16.7 us (24%)
  local copies, waits for them, and re-layouts  3.23 us (5%)
  other arithmetic  1.87 us (3%)
  between operations  1.41 us (2%)
    all_to_all x2, waiting for transfers between devices, fast_body(): block = lax.all_to_all(block, both, split_axis=0, concat_axis=0, tiled=True)  25.5 us
    all_to_all x2, starting transfers between devices, fast_body(): block = lax.all_to_all(block, both, split_axis=0, concat_axis=0, tiled=True)  9.95 us
    ppermute x4, starting transfers between devices, shift(): return lax.ppermute(value, axis, pairs)  9.18 us
    pallas_call x1, Pallas kernels, fast_body(): pl.pallas_call(functools.partial(middle_kernel, layers=layers), grid=(slo...  5.32 us
    pallas_call x1, Pallas kernels, fast_body(): pl.pallas_call(first_kernel, out_shape=[jax.ShapeDtypeStruct((3, rows, ce...  3.92 us
    pallas_call x1, Pallas kernels, fast_body(): pl.pallas_call(last_kernel, out_shape=[jax.ShapeDtypeStruct((3, rows, cel...  3.92 us
    unnamed x20, local copies, waits for them, and re-layouts  2.64 us
    pallas_call x1, Pallas kernels, fast_body(): pl.pallas_call(exchange_kernel, out_shape=jax.ShapeDtypeStruct((3, rows,...  2.42 us
  transfers between devices with their start and end apart: 6, of which 3 were waited for; matrix products, arithmetic and copies ran while one was open for 4% of the time, Pallas kernels for 5%

commit v1 on v0

--- a/solution.py
+++ b/solution.py
@@ -19,10 +19,12 @@
 sublanes = 8
 half = lanes // 2
 root_half = math.sqrt(0.5)
-chunk_count = 1
+piece_count = 4
 coef_count = 13
-both = ("layer", "plane")
+vmem_limit = 16 << 20
+both = ("plane", "layer")
 in_vmem = pl.BlockSpec(memory_space=pltpu.VMEM)
+in_any = pl.BlockSpec(memory_space=pl.ANY)
 in_smem = pl.BlockSpec(memory_space=pltpu.SMEM)
 
 
@@ -32,10 +34,12 @@
     return np.stack([head, rest])
 
 
-def row_table(cell_count):
-    turns = np.outer(np.arange(cell_count), np.arange(cell_count)) % (2 * cell_count)
-    phase = turns * (np.pi / cell_count)
-    return split_table(np.concatenate([np.cos(phase), -np.sin(phase)]))
+def edge_table():
+    slot, place = np.arange(half), np.arange(lanes)
+    zero = np.zeros((half, lanes))
+    phase = [2.0 * np.pi / (8 * lanes) * (np.outer(8 * slot + r, place) % (8 * lanes)) for r in (0, 4)]
+    rows = [np.block([[f(phase[0]), zero], [zero, f(phase[1])]]) for f in (np.cos, np.sin)]
+    return split_table(np.concatenate([rows[0], -rows[1]]))
 
 
 def short_tables():
@@ -74,36 +78,68 @@
     return angle * sine, cosine
 
 
-def first_kernel(polar_ref, azimuth_ref, saturation_ref, table_ref, moment_ref, head_ref, tail_ref, *out_refs):
-    rows, cell_count = polar_ref.shape
-    sin_polar, cos_polar = sine_cosine(polar_ref[...])
-    sin_half, cos_half = sine_cosine(0.5 * azimuth_ref[...])
+def first_kernel(
+    polar_hbm, azimuth_hbm, saturation_hbm, edge_hbm, back_hbm, twiddle_hbm, moment_hbm, side_hbm, out_hbm,
+    angle_ref, edge_ref, back_ref, twiddle_ref, moment_ref, side_ref, rows_ref, in_sem, out_sem,
+):
+    rows, cell_count = angle_ref.shape[1:]
+    sources = (polar_hbm, azimuth_hbm, saturation_hbm, edge_hbm, back_hbm, twiddle_hbm)
+    places = (angle_ref.at[0], angle_ref.at[1], angle_ref.at[2], edge_ref, back_ref, twiddle_ref)
+    loads = [
+        pltpu.make_async_copy(source, place, in_sem.at[n])
+        for n, (source, place) in enumerate(zip(sources, places))
+    ]
+    for copy in loads:
+        copy.start()
+    for copy in loads:
+        copy.wait()
+    sin_polar, cos_polar = sine_cosine(angle_ref[0])
+    sin_half, cos_half = sine_cosine(0.5 * angle_ref[1])
+    saturation = angle_ref[2]
     moment = (
         sin_polar * (1.0 - 2.0 * sin_half * sin_half),
         sin_polar * (2.0 * sin_half * cos_half),
         cos_polar,
     )
+    groups = [[] for _ in range(4)]
     for c in range(3):
         moment_ref[c] = moment[c]
-        head_ref[c : c + 1] = moment[c][:1]
-        tail_ref[c : c + 1] = moment[c][rows - 1 :]
-    saturation = saturation_ref[...]
-    magnet = [split(m * saturation) for m in moment]
-    blank = jnp.zeros((rows, cell_count), jnp.bfloat16)
-    for_real = [jnp.concatenate([m[n] for m in magnet] + [blank]) for n in range(2)]
-    for_imag = [jnp.concatenate([blank] + [m[n] for m in magnet]) for n in range(2)]
+        side_ref[0, c : c + 1] = moment[c][:1]
+        side_ref[1, c : c + 1] = moment[c][rows - 1 :]
+        magnet = moment[c] * saturation
+        a = [magnet[:, p * lanes : (p + 1) * lanes] for p in range(4)]
+        even, odd = a[0] + a[2], a[1] + a[3]
+        turned, mixed = root_half * (a[1] - a[3]), root_half * odd
+        groups[0].append((even + odd, even - odd))
+        for r, (real, imag) in (
+            (1, (a[0] + turned, -a[2] - mixed)),
+            (2, (a[0] - a[2], a[3] - a[1])),
+            (3, (a[0] - turned, a[2] - mixed)),
+        ):
+            cosine, sine = twiddle_ref[0, r, :1], twiddle_ref[1, r, :1]
+            groups[r].append((real * cosine + imag * sine, imag * cosine - real * sine))
+    blank = jnp.zeros((rows, 2 * lanes), jnp.bfloat16)
     dims = ((1,), (1,))
-    span = cell_count // len(out_refs)
-    for n, out_ref in enumerate(out_refs):
-        start = n * span
-        cosine = (table_ref[0, start : start + span], table_ref[1, start : start + span])
-        start += cell_count
-        sine = (table_ref[0, start : start + span], table_ref[1, start : start + span])
-        real = product(cosine, for_real, dims)
-        imag = product(sine, for_imag, dims)
-        out_ref[:, :lanes] = real[:, :lanes]
-        out_ref[:, lanes : 2 * lanes] = real[:, lanes:] + imag[:, :lanes]
-        out_ref[:, 2 * lanes :] = imag[:, lanes:]
+    for g in range(4):
+        parts = [split(jnp.concatenate(pair, axis=1)) for pair in groups[g]]
+        for_real = [jnp.concatenate([part[n] for part in parts] + [blank]) for n in range(2)]
+        for_imag = [jnp.concatenate([blank] + [part[n] for part in parts]) for n in range(2)]
+        table_ref = edge_ref if g == 0 else back_ref
+        real = product((table_ref[0, :lanes], table_ref[1, :lanes]), for_real, dims)
+        imag = product((table_ref[0, lanes:], table_ref[1, lanes:]), for_imag, dims)
+        cut = slice(g * lanes, (g + 1) * lanes)
+        rows_ref[cut, :lanes] = real[:, :lanes]
+        rows_ref[cut, lanes : 2 * lanes] = real[:, lanes:] + imag[:, :lanes]
+        rows_ref[cut, 2 * lanes :] = imag[:, lanes:]
+    sends = [
+        pltpu.make_async_copy(rows_ref, out_hbm, out_sem.at[0]),
+        pltpu.make_async_copy(moment_ref, moment_hbm, out_sem.at[1]),
+        pltpu.make_async_copy(side_ref, side_hbm, out_sem.at[2]),
+    ]
+    for copy in sends:
+        copy.start()
+    for copy in sends:
+        copy.wait()
 
 
 def factors(wave_x, wave_y):
@@ -124,41 +160,43 @@
     return unit_x, unit_y, self_part, mutual, decay
 
 
-def coef_kernel(base_ref, *out_refs, cell_count, span):
+def coef_kernel(base_ref, out_ref, *, cell_count):
     pad_length = 2 * cell_count
     radix = pad_length // lanes
     step = math.pi / side_length
-    for n, out_ref in enumerate(out_refs):
-        slots = out_ref.shape[2]
-        shape = (slots, lanes)
-        slot = n * span + base_ref[0] * slots + lax.broadcasted_iota(jnp.int32, shape, 0)
-        wave_y = step * slot.astype(jnp.float32)
-        weight = jnp.where(slot == 0, 1.0, 2.0) / float(pad_length * pad_length)
-        signed = jnp.where(slot % 2 == 0, weight, -weight)
-        for r in range(radix):
-            index = lax.broadcasted_iota(jnp.int32, shape, 1) * radix + r
-            middle = index == cell_count
-            folded = jnp.where(index < cell_count, index, index - pad_length)
-            wave_x = step * folded.astype(jnp.float32)
-            unit_x, unit_y, self_part, mutual, decay = factors(wave_x, wave_y)
-            out_ref[0, r] = jnp.where(middle, 0.0, unit_x)
-            out_ref[1, r] = unit_y
-            out_ref[2, r] = (1.0 - self_part) * weight
-            out_ref[3, r] = self_part * weight
-            out_ref[4, r] = mutual * weight
-            out_ref[5, r] = decay
-            edge = jnp.full(shape, -step * cell_count, jnp.float32)
-            edge_x, edge_y, self_part, mutual, decay = factors(wave_x, edge)
-            rest = (1.0 - self_part) * signed
-            mutual = mutual * signed
-            square = edge_y * edge_y
-            out_ref[6, r] = jnp.where(middle, 0.0, edge_x)
-            out_ref[7, r] = rest
-            out_ref[8, r] = self_part * signed
-            out_ref[9, r] = mutual
-            out_ref[10, r] = decay
-            out_ref[11, r] = rest * square
-            out_ref[12, r] = mutual * square
+    slots = out_ref.shape[2]
+    shape = (slots, lanes)
+    slot = base_ref[0] * slots + lax.broadcasted_iota(jnp.int32, shape, 0)
+    group, order = slot // lanes, slot % lanes
+    first = jnp.where(order < half, order * radix, (order - half) * radix + radix // 2)
+    wave = jnp.where(group == 0, first, order * radix + group)
+    wave_y = step * jnp.where(wave < cell_count, wave, wave - pad_length).astype(jnp.float32)
+    weight = jnp.where(wave == 0, 1.0, 2.0) / float(pad_length * pad_length)
+    signed = jnp.where(wave % 2 == 0, weight, -weight)
+    for r in range(radix):
+        index = lax.broadcasted_iota(jnp.int32, shape, 1) * radix + r
+        middle = index == cell_count
+        folded = jnp.where(index < cell_count, index, index - pad_length)
+        wave_x = step * folded.astype(jnp.float32)
+        unit_x, unit_y, self_part, mutual, decay = factors(wave_x, wave_y)
+        out_ref[0, r] = jnp.where(middle, 0.0, unit_x)
+        out_ref[1, r] = unit_y
+        out_ref[2, r] = (1.0 - self_part) * weight
+        out_ref[3, r] = self_part * weight
+        out_ref[4, r] = mutual * weight
+        out_ref[5, r] = decay
+        edge = jnp.full(shape, -step * cell_count, jnp.float32)
+        edge_x, edge_y, self_part, mutual, decay = factors(wave_x, edge)
+        rest = (1.0 - self_part) * signed
+        mutual = mutual * signed
+        square = edge_y * edge_y
+        out_ref[6, r] = jnp.where(middle, 0.0, edge_x)
+        out_ref[7, r] = rest
+        out_ref[8, r] = self_part * signed
+        out_ref[9, r] = mutual
+        out_ref[10, r] = decay
+        out_ref[11, r] = rest * square
+        out_ref[12, r] = mutual * square
 
 
 def neighbours(values, decay):
@@ -290,24 +328,25 @@
 def middle_kernel(rows_ref, coef_ref, twiddle_ref, forward_ref, back_ref, out_ref, work_ref, *, layers):
     radix = twiddle_ref.shape[1]
     pieces = radix // 2
-    planes = rows_ref.shape[0] // layers
     items = layers * 3
     place = lax.broadcasted_iota(jnp.int32, (sublanes, lanes), 1)
     low = place < half
-
-    def piece(row, part):
+    dims = ((1,), (0,))
+    forward = (forward_ref[0], forward_ref[1])
+    back = (back_ref[0], back_ref[1])
+
+    def piece(plane, layer, part):
         tile, upper = divmod(part, 2)
         cut = slice(tile * lanes, (tile + 1) * lanes)
-        first, second = rows_ref[row, :, cut], rows_ref[row + 1, :, cut]
+        row = plane * layers + layer
+        first, second = rows_ref[row, :, cut], rows_ref[row + layers, :, cut]
         if upper:
             return jnp.where(low, pltpu.roll(first, half, 1), second)
         return jnp.where(low, first, pltpu.roll(second, half, 1))
 
     for item in range(items):
         layer, c = divmod(item, 3)
-        z = [
-            (piece(layer * planes + 2 * p, c), piece(layer * planes + 2 * p, 3 + c)) for p in range(pieces)
-        ]
+        z = [(piece(2 * p, layer, c), piece(2 * p, layer, 3 + c)) for p in range(pieces)]
         for r, (real, imag) in enumerate(spread(z)):
             if r > 0:
                 cosine, sine = twiddle_ref[0, r], twiddle_ref[1, r]
@@ -315,9 +354,6 @@
             start = item * sublanes
             work_ref[r, start : start + sublanes, :lanes] = real
             work_ref[r, start : start + sublanes, lanes:] = imag
-    dims = ((1,), (0,))
-    forward = (forward_ref[0], forward_ref[1])
-    back = (back_ref[0], back_ref[1])
     for r in range(radix):
         value = product(split(work_ref[r]), forward, dims)
         spectrum = [
@@ -351,12 +387,12 @@
             for p, (real, imag) in enumerate(gather_back(v)):
                 parts[p][c], parts[p][3 + c] = real, imag
         for p in range(pieces):
-            row = layer * planes + 2 * p
             for tile in range(3):
                 first, second = parts[p][2 * tile], parts[p][2 * tile + 1]
                 cut = slice(tile * lanes, (tile + 1) * lanes)
+                row = 2 * p * layers + layer
                 out_ref[row, :, cut] = jnp.where(low, first, pltpu.roll(second, half, 1))
-                out_ref[row + 1, :, cut] = jnp.where(low, pltpu.roll(first, half, 1), second)
+                out_ref[row + layers, :, cut] = jnp.where(low, pltpu.roll(first, half, 1), second)
 
 
 def exchange_kernel(link_ref, moment_ref, below_ref, above_ref, before_ref, after_ref, anisotropy_ref, out_ref):
@@ -377,36 +413,51 @@
         out_ref[c] = total
 
 
-def inverse_rows(block_refs, table_ref, cell_count, rows):
-    span = cell_count // len(block_refs)
+def last_kernel(
+    moment_ref, other_ref, edge_ref, back_ref, twiddle_ref, block_ref, field_ref, out_ref
+):
+    rows = moment_ref.shape[1]
+    turned = block_ref[...].T
     dims = ((1,), (0,))
-    total = None
-    for n, block_ref in enumerate(block_refs):
-        turned = block_ref[...].T
-        for part in range(2):
-            start = part * cell_count + n * span
-            table = (table_ref[0, start : start + span], table_ref[1, start : start + span])
-            term = product(split(turned[part * 3 * rows : (part + 1) * 3 * rows]), table, dims)
-            total = term if total is None else total + term
-    return total
-
-
-def last_kernel(moment_ref, other_ref, table_ref, *refs):
-    block_refs, (field_ref, out_ref) = refs[:-2], refs[-2:]
-    rows, cell_count = moment_ref.shape[1:]
-    demag = inverse_rows(block_refs, table_ref, cell_count, rows)
-    m = [moment_ref[c] for c in range(3)]
-    f = [other_ref[c] + demag[c * rows : (c + 1) * rows] for c in range(3)]
-    first = cross(m, f)
-    second = cross(m, first)
-    stepped = []
-    for c in range(3):
-        field_ref[c] = f[c]
-        torque = -(first[c] + damping * second[c]) / (1.0 + damping * damping)
-        stepped.append(m[c] + time_step * torque)
-    scale = lax.rsqrt(stepped[0] * stepped[0] + stepped[1] * stepped[1] + stepped[2] * stepped[2])
-    for c in range(3):
-        out_ref[c] = stepped[c] * scale
+    waves = []
+    for g in range(4):
+        cut = slice(g * lanes, (g + 1) * lanes)
+        value = jnp.concatenate([turned[: 3 * rows, cut], turned[3 * rows :, cut]], axis=1)
+        table_ref = edge_ref if g == 0 else back_ref
+        value = product(split(value), (table_ref[0], table_ref[1]), dims)
+        real, imag = value[:, :lanes], value[:, lanes:]
+        if g > 0:
+            cosine, sine = twiddle_ref[0, g, :1], twiddle_ref[1, g, :1]
+            real, imag = real * cosine - imag * sine, imag * cosine + real * sine
+        waves.append((real, imag))
+    even, odd = waves[0][0] + waves[0][1], waves[0][0] - waves[0][1]
+    (real_1, imag_1), (real_2, imag_2), (real_3, imag_3) = waves[1:]
+    flat, tilted = root_half * (real_1 - real_3), root_half * (imag_1 + imag_3)
+    demag = jnp.concatenate(
+        [
+            even + real_1 + real_2 + real_3,
+            odd + flat - tilted - imag_2,
+            even - imag_1 - real_2 + imag_3,
+            odd - flat - tilted + imag_2,
+        ],
+        axis=1,
+    )
+    span = rows // piece_count
+    for n in range(piece_count):
+        cut = pl.ds(n * span, span)
+        m = [moment_ref[c, cut] for c in range(3)]
+        f = [other_ref[c, cut] + demag[c * rows + n * span : c * rows + (n + 1) * span] for c in range(3)]
+        for c in range(3):
+            field_ref[c, cut] = f[c]
+        first = cross(m, f)
+        second = cross(m, first)
+        stepped = []
+        for c in range(3):
+            torque = -(first[c] + damping * second[c]) / (1.0 + damping * damping)
+            stepped.append(m[c] + time_step * torque)
+        scale = lax.rsqrt(stepped[0] * stepped[0] + stepped[1] * stepped[1] + stepped[2] * stepped[2])
+        for c in range(3):
+            out_ref[c, cut] = stepped[c] * scale
 
 
 def cross(first, second):
@@ -429,45 +480,55 @@
     device_count = layers * planes
     layer_index = lax.axis_index("layer")
     plane_index = lax.axis_index("plane")
-    span = cell_count // chunk_count
-    slots = span // device_count
+    slots = cell_count // device_count
     radix = 2 * cell_count // lanes
     width = 6 * rows
-    f32 = jnp.float32
-    table = jnp.asarray(row_table(cell_count))
+    f32, bf16 = jnp.float32, jnp.bfloat16
+    edge = jnp.asarray(edge_table())
     forward, back = (jnp.asarray(t) for t in short_tables())
     twiddle = jnp.asarray(twiddle_table(radix))
-
-    moment, top, bottom, *sent = pl.pallas_call(
+    field_shape = jax.ShapeDtypeStruct((3, rows, cell_count), f32)
+    side_shape = (2, sublanes, cell_count)
+    block_shape = jax.ShapeDtypeStruct((cell_count, width), f32)
+    small = pltpu.CompilerParams(vmem_limit_bytes=vmem_limit)
+    dma = pltpu.SemaphoreType.DMA
+    flops = 12 * rows * cell_count * cell_count * 6
+
+    moment, side, block = pl.pallas_call(
         first_kernel,
-        out_shape=[
-            jax.ShapeDtypeStruct((3, rows, cell_count), f32),
-            jax.ShapeDtypeStruct((sublanes, cell_count), f32),
-            jax.ShapeDtypeStruct((sublanes, cell_count), f32),
-        ]
-        + [jax.ShapeDtypeStruct((span, width), f32)] * chunk_count,
-        in_specs=[in_vmem] * 4,
-        out_specs=[in_vmem] * (3 + chunk_count),
-        cost_estimate=pl.CostEstimate(
-            flops=12 * rows * cell_count * cell_count * 6, bytes_accessed=8 << 20, transcendentals=0
-        ),
+        out_shape=[field_shape, jax.ShapeDtypeStruct(side_shape, f32), block_shape],
+        in_specs=[in_any] * 6,
+        out_specs=[in_any] * 3,
+        scratch_shapes=[
+            pltpu.VMEM((3, rows, cell_count), f32),
+            pltpu.VMEM(edge.shape, bf16),
+            pltpu.VMEM(back.shape, bf16),
+            pltpu.VMEM(twiddle.shape, f32),
+            pltpu.VMEM((3, rows, cell_count), f32),
+            pltpu.VMEM(side_shape, f32),
+            pltpu.VMEM((cell_count, width), f32),
+            dma((6,)),
+            dma((3,)),
+        ],
+        cost_estimate=pl.CostEstimate(flops=flops, bytes_accessed=4 << 20, transcendentals=0),
         name="first",
-    )(polar[0], azimuth[0], saturation[0], table)
-
-    base = (layer_index * planes + plane_index).astype(jnp.int32).reshape(1)
+    )(polar[0], azimuth[0], saturation[0], edge, back, twiddle)
+
+    base = (plane_index * layers + layer_index).astype(jnp.int32).reshape(1)
     coefs = pl.pallas_call(
-        functools.partial(coef_kernel, cell_count=cell_count, span=span),
-        out_shape=[jax.ShapeDtypeStruct((coef_count, radix, slots, lanes), f32)] * chunk_count,
+        functools.partial(coef_kernel, cell_count=cell_count),
+        out_shape=jax.ShapeDtypeStruct((coef_count, radix, slots, lanes), f32),
         in_specs=[in_smem],
-        out_specs=[in_vmem] * chunk_count,
+        out_specs=in_vmem,
+        compiler_params=small,
         cost_estimate=pl.CostEstimate(flops=20 << 20, bytes_accessed=1 << 20, transcendentals=1 << 16),
         name="coefs",
     )(base)
 
     below = shift(moment, "layer", 1)
     above = shift(moment, "layer", -1)
-    before = shift(bottom, "plane", 1)
-    after = shift(top, "plane", -1)
+    before = shift(side[1], "plane", 1)
+    after = shift(side[0], "plane", -1)
     links = jnp.stack(
         [
             stiffness[0],
@@ -477,46 +538,46 @@
     )
     other = pl.pallas_call(
         exchange_kernel,
-        out_shape=jax.ShapeDtypeStruct((3, rows, cell_count), f32),
+        out_shape=field_shape,
         in_specs=[in_smem] + [in_vmem] * 6,
         out_specs=in_vmem,
+        compiler_params=small,
         cost_estimate=pl.CostEstimate(flops=20 << 20, bytes_accessed=2 << 20, transcendentals=0),
         name="exchange",
     )(links, moment, below, above, before, after, anisotropy[0])
 
-    received = []
-    for n in range(chunk_count):
-        block = sent[n].reshape(device_count, slots, width)
-        block = lax.all_to_all(block, both, split_axis=0, concat_axis=0, tiled=True)
-        block = pl.pallas_call(
-            functools.partial(middle_kernel, layers=layers),
-            grid=(slots // sublanes,),
-            out_shape=jax.ShapeDtypeStruct((device_count, slots, width), f32),
-            in_specs=[
-                pl.BlockSpec((device_count, sublanes, width), lambda g: (0, g, 0)),
-                pl.BlockSpec((coef_count, radix, sublanes, lanes), lambda g: (0, 0, g, 0)),
-                pl.BlockSpec((2, radix, sublanes, lanes), lambda g: (0, 0, 0, 0)),
-                pl.BlockSpec((2, 2 * lanes, 2 * lanes), lambda g: (0, 0, 0)),
-                pl.BlockSpec((2, 2 * lanes, 2 * lanes), lambda g: (0, 0, 0)),
-            ],
-            out_specs=pl.BlockSpec((device_count, sublanes, width), lambda g: (0, g, 0)),
-            scratch_shapes=[pltpu.VMEM((radix, layers * 3 * sublanes, 2 * lanes), f32)],
-            cost_estimate=pl.CostEstimate(flops=2000 << 20, bytes_accessed=4 << 20, transcendentals=0),
-            name="middle",
-        )(block, coefs[n], twiddle, forward, back)
-        block = lax.all_to_all(block, both, split_axis=0, concat_axis=0, tiled=True)
-        received.append(block.reshape(span, width))
+    exchange_all = functools.partial(
+        lax.all_to_all, axis_name=both, split_axis=0, concat_axis=0, tiled=True
+    )
+    block = exchange_all(block.reshape(device_count, slots, width))
+    block = pl.pallas_call(
+        functools.partial(middle_kernel, layers=layers),
+        out_shape=jax.ShapeDtypeStruct((device_count, slots, width), f32),
+        grid=(slots // sublanes,),
+        in_specs=[
+            pl.BlockSpec((device_count, sublanes, width), lambda g: (0, g, 0)),
+            pl.BlockSpec((coef_count, radix, sublanes, lanes), lambda g: (0, 0, g, 0)),
+            pl.BlockSpec(twiddle.shape, lambda g: (0, 0, 0, 0)),
+            pl.BlockSpec(forward.shape, lambda g: (0, 0, 0)),
+            pl.BlockSpec(back.shape, lambda g: (0, 0, 0)),
+        ],
+        out_specs=pl.BlockSpec((device_count, sublanes, width), lambda g: (0, g, 0)),
+        scratch_shapes=[pltpu.VMEM((radix, layers * 3 * sublanes, 2 * lanes), f32)],
+        compiler_params=small,
+        cost_estimate=pl.CostEstimate(flops=2000 << 20, bytes_accessed=4 << 20, transcendentals=0),
+        name="middle",
+    )(block, coefs, twiddle, forward, back)
+    block = exchange_all(block)
 
     field, stepped = pl.pallas_call(
         last_kernel,
-        out_shape=[jax.ShapeDtypeStruct((3, rows, cell_count), f32)] * 2,
-        in_specs=[in_vmem] * (3 + chunk_count),
+        out_shape=[field_shape] * 2,
+        in_specs=[in_vmem] * 6,
         out_specs=[in_vmem] * 2,
-        cost_estimate=pl.CostEstimate(
-            flops=12 * rows * cell_count * cell_count * 6, bytes_accessed=8 << 20, transcendentals=0
-        ),
+        compiler_params=small,
+        cost_estimate=pl.CostEstimate(flops=flops, bytes_accessed=4 << 20, transcendentals=0),
         name="last",
-    )(moment, other, table, *received)
+    )(moment, other, edge, back, twiddle, block.reshape(cell_count, width))
     return field[None], stepped[None]
 
 
@@ -677,7 +738,7 @@
     rows, cell_count = polar.shape[1:]
     device_count = lax.axis_size("layer") * lax.axis_size("plane")
     fits = 2 * rows == lanes and cell_count == 4 * lanes
-    fits = fits and cell_count % (chunk_count * device_count * sublanes) == 0
+    fits = fits and cell_count % (device_count * sublanes) == 0
     chosen = fast_body if fits else plain_body
     return chosen(polar, azimuth, saturation, anisotropy, stiffness, coupling)
 

time: 69.7 us -> 62.8 us (0.901)
  Pallas kernels: 16.7 us -> 10.5 us
  local copies, waits for them, and re-layouts: 3.23 us -> 0.64 us
  starting transfers between devices: 19.1 us -> 21.1 us
    pallas_call x5, Pallas kernels: 16.7 us -> 10.5 us  [the longest x1 4.14 us: fast_body(): pl.pallas_call(functools.partial(middle_kernel, layers=layers), out_shape...]
    unnamed x20 -> x16, local copies, waits for them, and re-layouts: 2.64 us -> 0.04 us
    all_to_all x2, waiting for transfers between devices: 25.5 us -> 27.2 us  [the longest x1 20.3 us: fast_body(): block = exchange_all(block.reshape(device_count, slots, width))]
    ppermute x4, waiting for transfers between devices: 1.41 us -> 0.01 us  [shift(): return lax.ppermute(value, axis, pairs)]
    all_to_all x2, starting transfers between devices: 9.95 us -> 11 us  [the longest x1 7.33 us: fast_body(): block = exchange_all(block.reshape(device_count, slots, width))]
    ppermute x4, starting transfers between devices: 9.18 us -> 10.2 us  [shift(): return lax.ppermute(value, axis, pairs)]
  transfers between devices with their start and end apart: 6 -> 6, of which waited for: 3 -> 2; matrix products, arithmetic and copies ran while one was open for 4% -> 3% of each run, Pallas kernels for 5% -> 2%
where the time goes in v1:
time: 62.8 us; the launch traced here: 62.4 us
  waiting for transfers between devices  27.3 us (43%)
  starting transfers between devices  21.1 us (34%)
  Pallas kernels  10.5 us (17%)
  between operations  1.46 us (2%)
  other arithmetic  1.37 us (2%)
  local copies, waits for them, and re-layouts  0.64 us (1%)
    all_to_all x1, waiting for transfers between devices, fast_body(): block = exchange_all(block.reshape(device_count, slots, width))  20.3 us
    ppermute x4, starting transfers between devices, shift(): return lax.ppermute(value, axis, pairs)  10.2 us
    all_to_all x1, starting transfers between devices, fast_body(): block = exchange_all(block.reshape(device_count, slots, width))  7.33 us
    all_to_all x1, waiting for transfers between devices, fast_body(): block = exchange_all(block)  6.96 us
    pallas_call x1, Pallas kernels, fast_body(): pl.pallas_call(functools.partial(middle_kernel, layers=layers), out_shape...  4.14 us
    all_to_all x1, starting transfers between devices, fast_body(): block = exchange_all(block)  3.63 us
    pallas_call x1, Pallas kernels, fast_body(): pl.pallas_call(first_kernel, out_shape=[field_shape, jax.ShapeDtypeStruct...  3.55 us
    pallas_call x1, Pallas kernels, fast_body(): pl.pallas_call(last_kernel, out_shape=[field_shape] * 2, in_specs=[in_vme...  1.7 us
  transfers between devices with their start and end apart: 6, of which 2 were waited for; matrix products, arithmetic and copies ran while one was open for 3% of the time, Pallas kernels for 2%

profile of v1, /device:TPU:0, one launch (start us, length us, event | category | flops | bytes accessed | tf_op | source)
XLA Modules:
  0.0 62.4 jit_solution(9012714573450829266)
XLA Ops:
  0.6 3.5 %first.1 = (f32[3,64,512]{2,1,0:T(8,128)}, f32[2,8,512]{2,1,0:T(8,128)}, f32[512,384]{1,0:T(8,128)}) custom-call(f32[64,512]{1,0:T(8,128)} %bitcast.16, f32[64,512]{1,0:T(8,128)} %bitcast.17, f32[64,512]{1,0:T(8,128)} %bitcast.18, bf16[2,256,256]{2,1,0:T(8,128)(2,1)} %constant.28.clone.edge_hbm.edge_ref, ...), custom_call_target="tpu_custom_call" | custom-call | flops 1207959552 | bytes 4194304 | tf_op jit(solution)/shard_map/first/pallas_call | solution.py:497
  4.2 7.3 %all-to-all-start = ((f32[32,16,384]{2,1,0:T(8,128)}), f32[32,16,384]{2,1,0:T(8,128)S(1)}, u32[]{:S(2)}, u32[]{:S(2)}) async-start(f32[32,16,384]{2,1,0:T(8,128)} %bitcast.15), calls=%async_computation | async-start | bytes 1572864 | tf_op jit(solution)/shard_map/all_to_all | solution.py:552
  11.5 0.0 copy-start.2
  11.5 0.0 copy-start.4
  11.6 0.0 copy-start.5
  11.6 0.3 coefs.1.coef_ref
  11.8 20.3 %all-to-all-done.rows_ref = f32[32,16,384]{2,1,0:T(8,128)S(1)} async-done(((f32[32,16,384]{2,1,0:T(8,128)}), f32[32,16,384]{2,1,0:T(8,128)S(1)}, u32[]{:S(2)}, u32[]{:S(2)}) %all-to-all-start) | async-done | bytes 786464 | tf_op jit(solution)/shard_map/all_to_all | solution.py:552
  32.1 0.0 copy-done.2
  32.1 0.0 copy-done.4
  32.1 0.0 copy-done.5
  32.1 4.1 %middle.1 = f32[32,16,384]{2,1,0:T(8,128)} custom-call(f32[32,16,384]{2,1,0:T(8,128)S(1)} %all-to-all-done.rows_ref, f32[13,8,16,128]{3,2,1,0:T(8,128)S(1)} %coefs.1.coef_ref, f32[2,8,8,128]{3,2,1,0:T(8,128)S(1)} %copy-done.5, bf16[2,256,256]{2,1,0:T(8,128)(2,1)S(1)} %copy-done.4, bf16[2,256,256]{2,1,0:T(8,128)(2,1)S(1)} %copy-done.2), custom_call_target="tpu_custom_call" | custom-call | flops 2097152000 | bytes 4194304 | tf_op jit(solution)/shard_map/middle/pallas_call | solution.py:553
  36.3 0.0 copy-start
  36.3 3.6 %all-to-all-start.1 = ((f32[32,16,384]{2,1,0:T(8,128)}), f32[32,16,384]{2,1,0:T(8,128)S(1)}, u32[]{:S(2)}, u32[]{:S(2)}) async-start(f32[32,16,384]{2,1,0:T(8,128)} %middle.1), calls=%async_computation.1 | async-start | bytes 1572864 | tf_op jit(solution)/shard_map/all_to_all | solution.py:570
  39.9 0.0 copy-done
  39.9 1.3 %collective-permute-start.1 = (f32[3,64,512]{2,1,0:T(8,128)S(1)}, f32[3,64,512]{2,1,0:T(8,128)S(1)}, u32[]{:S(2)}, u32[]{:S(2)}) collective-permute-start(f32[3,64,512]{2,1,0:T(8,128)S(1)} %copy-done), channel_id=1, source_target_pairs={{8,0},{16,8},{24,16},{9,1},{17,9},{25,17},{10,2},{18,10},{26,18},{... | collective-permute-start | bytes 1179656 | tf_op jit(solution)/shard_map/ppermute | solution.py:474
  41.2 3.1 %collective-permute-start = (f32[3,64,512]{2,1,0:T(8,128)S(1)}, f32[3,64,512]{2,1,0:T(8,128)S(1)}, u32[]{:S(2)}, u32[]{:S(2)}) collective-permute-start(f32[3,64,512]{2,1,0:T(8,128)S(1)} %copy-done), channel_id=1, source_target_pairs={{0,8},{8,16},{16,24},{1,9},{9,17},{17,25},{2,10},{10,18},{18,26},{... | collective-permute-start | bytes 1179656 | tf_op jit(solution)/shard_map/ppermute | solution.py:474
  44.3 0.0 copy-done.6
  44.3 1.3 %collective-permute-start.3 = (f32[8,512]{1,0:T(8,128)S(1)}, f32[8,512]{1,0:T(8,128)S(1)}, u32[]{:S(2)}, u32[]{:S(2)}) collective-permute-start(f32[8,512]{1,0:T(8,128)S(1)} %get-tuple-element.12), channel_id=1, source_target_pairs={{1,0},{2,1},{3,2},{4,3},{5,4},{6,5},{7,6},{9,8},{10,9},{11,10},{12... | collective-permute-start | bytes 49160 | tf_op jit(solution)/shard_map/ppermute | solution.py:474
  45.6 4.5 %collective-permute-start.2 = (f32[8,512]{1,0:T(8,128)S(1)}, f32[8,512]{1,0:T(8,128)S(1)}, u32[]{:S(2)}, u32[]{:S(2)}) collective-permute-start(f32[8,512]{1,0:T(8,128)S(1)} %get-tuple-element.13), channel_id=1, source_target_pairs={{0,1},{1,2},{2,3},{3,4},{4,5},{5,6},{6,7},{8,9},{9,10},{10,11},{11... | collective-permute-start | bytes 49160 | tf_op jit(solution)/shard_map/ppermute | solution.py:474
  50.8 0.0 copy-done.7
  50.8 0.6 fusion
  51.4 1.4 %pad_maximum_fusion.link_ref = f32[3]{0:T(128)S(1)} fusion(f32[1]{0:T(128)} %get-tuple-element.15, f32[1]{0:T(128)} %get-tuple-element.14, f32[1]{0:T(128)S(6)} %copy.12), kind=kLoop, calls=%fused_computation.2 | loop fusion | flops 6 | bytes 24 | tf_op jit(solution)/shard_map/stack | solution.py:532
  52.8 0.0 collective-permute-done.3.after_ref
  52.8 0.0 collective-permute-done.2.before_ref
  52.8 0.0 collective-permute-done.1.above_ref
  52.8 0.0 collective-permute-done.below_ref
  52.8 0.0 copy-done.1
  52.8 0.0 copy-start.3
  52.8 0.9 %exchange.1.other_ref = f32[3,64,512]{2,1,0:T(8,128)S(1)} custom-call(f32[3]{0:T(128)S(1)} %pad_maximum_fusion.link_ref, f32[3,64,512]{2,1,0:T(8,128)S(1)} %copy-done, f32[3,64,512]{2,1,0:T(8,128)S(1)} %collective-permute-done.below_ref, f32[3,64,512]{2,1,0:T(8,128)S(1)} %collective-permute-done.1.above_ref, f32[8,512]{1,0:T(8,128)S(1)} %collective-permute-done.2.before_ref, ...), custom_call_target="tpu_custom_call" | custom-call | flops 20971520 | bytes 2097152 | tf_op jit(solution)/shard_map/exchange/pallas_call | solution.py:539
  53.7 7.0 %all-to-all-done.1 = f32[32,16,384]{2,1,0:T(8,128)S(1)} async-done(((f32[32,16,384]{2,1,0:T(8,128)}), f32[32,16,384]{2,1,0:T(8,128)S(1)}, u32[]{:S(2)}, u32[]{:S(2)}) %all-to-all-start.1) | async-done | bytes 786464 | tf_op jit(solution)/shard_map/all_to_all | solution.py:570
  60.7 0.0 copy-done.3
  60.7 1.7 %last.1 = (f32[3,64,512]{2,1,0:T(8,128)}, f32[3,64,512]{2,1,0:T(8,128)}) custom-call(f32[3,64,512]{2,1,0:T(8,128)S(1)} %copy-done, f32[3,64,512]{2,1,0:T(8,128)S(1)} %exchange.1.other_ref, bf16[2,256,256]{2,1,0:T(8,128)(2,1)S(1)} %copy-done.3, bf16[2,256,256]{2,1,0:T(8,128)(2,1)S(1)} %copy-done.2, f32[2,8,8,128]{3,2,1,0:T(8,128)S(1)} %copy-done.5, ...), custom_call_target="tpu_custom_call" | custom-call | flops 1207959552 | bytes 4194304 | tf_op jit(solution)/shard_map/last/pallas_call | solution.py:572
  (4 shorter events, 0.0 us)
Async XLA Ops:
  4.2 27.9 %all-to-all-start = ((f32[32,16,384]{2,1,0:T(8,128)}), f32[32,16,384]{2,1,0:T(8,128)S(1)}, u32[]{:S(2)}, u32[]{:S(2)}) async-start(f32[32,16,384]{2,1,0:T(8,128)} %bitcast.15), calls=%async_computation | async-start | bytes 1572864 | tf_op jit(solution)/shard_map/all_to_all | solution.py:552
  11.5 20.6 %copy-start.2 = (bf16[2,256,256]{2,1,0:T(8,128)(2,1)S(1)}, bf16[2,256,256]{2,1,0:T(8,128)(2,1)}, u32[]{:S(2)}) copy-start(bf16[2,256,256]{2,1,0:T(8,128)(2,1)} %constant.30.clone.back_hbm.back_ref) | copy-start | bytes 786436
  11.5 20.6 %copy-start.4 = (bf16[2,256,256]{2,1,0:T(8,128)(2,1)S(1)}, bf16[2,256,256]{2,1,0:T(8,128)(2,1)}, u32[]{:S(2)}) copy-start(bf16[2,256,256]{2,1,0:T(8,128)(2,1)} %constant.29.clone.forward_ref) | copy-start | bytes 786436
  11.6 20.6 %copy-start.5 = (f32[2,8,8,128]{3,2,1,0:T(8,128)S(1)}, f32[2,8,8,128]{3,2,1,0:T(8,128)}, u32[]{:S(2)}) copy-start(f32[2,8,8,128]{3,2,1,0:T(8,128)} %constant.31.clone.twiddle_hbm.twiddle_ref) | copy-start | bytes 196612
  36.3 3.6 %copy-start = (f32[3,64,512]{2,1,0:T(8,128)S(1)}, f32[3,64,512]{2,1,0:T(8,128)}, u32[]{:S(2)}) copy-start(f32[3,64,512]{2,1,0:T(8,128)} %get-tuple-element.7.moment_ref) | copy-start | bytes 1179652
  36.3 8.0 %copy-start.6 = (f32[2,8,512]{2,1,0:T(8,128)S(1)}, f32[2,8,512]{2,1,0:T(8,128)}, u32[]{:S(2)}) copy-start(f32[2,8,512]{2,1,0:T(8,128)} %get-tuple-element.8) | copy-start | bytes 98308
  36.3 14.6 %copy-start.7 = (f32[3]{0:T(128)S(1)}, f32[3]{0:T(128)}, u32[]{:S(2)}) copy-start(f32[3]{0:T(128)} %param.15) | copy-start | bytes 40
  36.3 16.5 %copy-start.1 = (f32[1,64,512]{2,1,0:T(8,128)S(1)}, f32[1,64,512]{2,1,0:T(8,128)}, u32[]{:S(2)}) copy-start(f32[1,64,512]{2,1,0:T(8,128)} %param.13) | copy-start | bytes 393220
  36.3 24.4 %all-to-all-start.1 = ((f32[32,16,384]{2,1,0:T(8,128)}), f32[32,16,384]{2,1,0:T(8,128)S(1)}, u32[]{:S(2)}, u32[]{:S(2)}) async-start(f32[32,16,384]{2,1,0:T(8,128)} %middle.1), calls=%async_computation.1 | async-start | bytes 1572864 | tf_op jit(solution)/shard_map/all_to_all | solution.py:570
  39.9 12.9 %collective-permute-start.1 = (f32[3,64,512]{2,1,0:T(8,128)S(1)}, f32[3,64,512]{2,1,0:T(8,128)S(1)}, u32[]{:S(2)}, u32[]{:S(2)}) collective-permute-start(f32[3,64,512]{2,1,0:T(8,128)S(1)} %copy-done), channel_id=1, source_target_pairs={{8,0},{16,8},{24,16},{9,1},{17,9},{25,17},{10,2},{18,10},{26,18},{... | collective-permute-start | bytes 1179656 | tf_op jit(solution)/shard_map/ppermute | solution.py:474
  41.2 11.6 %collective-permute-start = (f32[3,64,512]{2,1,0:T(8,128)S(1)}, f32[3,64,512]{2,1,0:T(8,128)S(1)}, u32[]{:S(2)}, u32[]{:S(2)}) collective-permute-start(f32[3,64,512]{2,1,0:T(8,128)S(1)} %copy-done), channel_id=1, source_target_pairs={{0,8},{8,16},{16,24},{1,9},{9,17},{17,25},{2,10},{10,18},{18,26},{... | collective-permute-start | bytes 1179656 | tf_op jit(solution)/shard_map/ppermute | solution.py:474
  44.3 8.5 %collective-permute-start.3 = (f32[8,512]{1,0:T(8,128)S(1)}, f32[8,512]{1,0:T(8,128)S(1)}, u32[]{:S(2)}, u32[]{:S(2)}) collective-permute-start(f32[8,512]{1,0:T(8,128)S(1)} %get-tuple-element.12), channel_id=1, source_target_pairs={{1,0},{2,1},{3,2},{4,3},{5,4},{6,5},{7,6},{9,8},{10,9},{11,10},{12... | collective-permute-start | bytes 49160 | tf_op jit(solution)/shard_map/ppermute | solution.py:474
  45.6 7.2 %collective-permute-start.2 = (f32[8,512]{1,0:T(8,128)S(1)}, f32[8,512]{1,0:T(8,128)S(1)}, u32[]{:S(2)}, u32[]{:S(2)}) collective-permute-start(f32[8,512]{1,0:T(8,128)S(1)} %get-tuple-element.13), channel_id=1, source_target_pairs={{0,1},{1,2},{2,3},{3,4},{4,5},{5,6},{6,7},{8,9},{9,10},{10,11},{11... | collective-permute-start | bytes 49160 | tf_op jit(solution)/shard_map/ppermute | solution.py:474
  52.8 7.9 %copy-start.3 = (bf16[2,256,256]{2,1,0:T(8,128)(2,1)S(1)}, bf16[2,256,256]{2,1,0:T(8,128)(2,1)}, u32[]{:S(2)}) copy-start(bf16[2,256,256]{2,1,0:T(8,128)(2,1)} %constant.28.clone.edge_hbm.edge_ref) | copy-start | bytes 786436

commit v2 on v1

--- a/solution.py
+++ b/solution.py
@@ -19,8 +19,8 @@
 sublanes = 8
 half = lanes // 2
 root_half = math.sqrt(0.5)
-piece_count = 4
-coef_count = 13
+piece_count = 2
+coef_count = 6
 vmem_limit = 16 << 20
 both = ("plane", "layer")
 in_vmem = pl.BlockSpec(memory_space=pltpu.VMEM)
@@ -61,10 +61,13 @@
 
 
 def product(left, right, dims):
-    dot = functools.partial(
-        lax.dot_general, dimension_numbers=(dims, ((), ())), preferred_element_type=jnp.float32
-    )
-    return dot(left[0], right[0]) + (dot(left[1], right[0]) + dot(left[0], right[1]))
+    (axis,), (other,) = dims
+    return lax.dot_general(
+        jnp.concatenate([left[0], left[1], left[0]], axis=axis),
+        jnp.concatenate([right[0], right[0], right[1]], axis=other),
+        dimension_numbers=(dims, ((), ())),
+        preferred_element_type=jnp.float32,
+    )
 
 
 def sine_cosine(angle):
@@ -118,6 +121,12 @@
         ):
             cosine, sine = twiddle_ref[0, r, :1], twiddle_ref[1, r, :1]
             groups[r].append((real * cosine + imag * sine, imag * cosine - real * sine))
+    sends = [
+        pltpu.make_async_copy(moment_ref, moment_hbm, out_sem.at[0]),
+        pltpu.make_async_copy(side_ref, side_hbm, out_sem.at[1]),
+    ]
+    for copy in sends:
+        copy.start()
     blank = jnp.zeros((rows, 2 * lanes), jnp.bfloat16)
     dims = ((1,), (1,))
     for g in range(4):
@@ -131,13 +140,8 @@
         rows_ref[cut, :lanes] = real[:, :lanes]
         rows_ref[cut, lanes : 2 * lanes] = real[:, lanes:] + imag[:, :lanes]
         rows_ref[cut, 2 * lanes :] = imag[:, lanes:]
-    sends = [
-        pltpu.make_async_copy(rows_ref, out_hbm, out_sem.at[0]),
-        pltpu.make_async_copy(moment_ref, moment_hbm, out_sem.at[1]),
-        pltpu.make_async_copy(side_ref, side_hbm, out_sem.at[2]),
-    ]
-    for copy in sends:
-        copy.start()
+        sends.append(pltpu.make_async_copy(rows_ref.at[cut], out_hbm.at[cut], out_sem.at[2 + g]))
+        sends[-1].start()
     for copy in sends:
         copy.wait()
 
@@ -160,7 +164,11 @@
     return unit_x, unit_y, self_part, mutual, decay
 
 
-def coef_kernel(base_ref, out_ref, *, cell_count):
+def coef_kernel(base_ref, *refs, cell_count):
+    count = len(refs) // 2 - 1
+    out_ref, edge_ref, sign_ref = refs[count : count + 3]
+    for table_ref, kept_ref in zip(refs[:count], refs[count + 3 :]):
+        kept_ref[...] = table_ref[...]
     pad_length = 2 * cell_count
     radix = pad_length // lanes
     step = math.pi / side_length
@@ -172,31 +180,28 @@
     wave = jnp.where(group == 0, first, order * radix + group)
     wave_y = step * jnp.where(wave < cell_count, wave, wave - pad_length).astype(jnp.float32)
     weight = jnp.where(wave == 0, 1.0, 2.0) / float(pad_length * pad_length)
-    signed = jnp.where(wave % 2 == 0, weight, -weight)
+    sign_ref[...] = jnp.where(wave % 2 == 0, weight, -weight)
     for r in range(radix):
         index = lax.broadcasted_iota(jnp.int32, shape, 1) * radix + r
-        middle = index == cell_count
         folded = jnp.where(index < cell_count, index, index - pad_length)
-        wave_x = step * folded.astype(jnp.float32)
-        unit_x, unit_y, self_part, mutual, decay = factors(wave_x, wave_y)
-        out_ref[0, r] = jnp.where(middle, 0.0, unit_x)
+        unit_x, unit_y, self_part, mutual, decay = factors(step * folded.astype(jnp.float32), wave_y)
+        out_ref[0, r] = jnp.where(index == cell_count, 0.0, unit_x)
         out_ref[1, r] = unit_y
         out_ref[2, r] = (1.0 - self_part) * weight
         out_ref[3, r] = self_part * weight
         out_ref[4, r] = mutual * weight
         out_ref[5, r] = decay
-        edge = jnp.full(shape, -step * cell_count, jnp.float32)
-        edge_x, edge_y, self_part, mutual, decay = factors(wave_x, edge)
-        rest = (1.0 - self_part) * signed
-        mutual = mutual * signed
-        square = edge_y * edge_y
-        out_ref[6, r] = jnp.where(middle, 0.0, edge_x)
-        out_ref[7, r] = rest
-        out_ref[8, r] = self_part * signed
-        out_ref[9, r] = mutual
-        out_ref[10, r] = decay
-        out_ref[11, r] = rest * square
-        out_ref[12, r] = mutual * square
+    shape = (radix, lanes)
+    index = lax.broadcasted_iota(jnp.int32, shape, 1) * radix + lax.broadcasted_iota(jnp.int32, shape, 0)
+    folded = jnp.where(index < cell_count, index, index - pad_length)
+    wave_y = jnp.full(shape, -step * cell_count, jnp.float32)
+    edge_x, edge_y, self_part, mutual, decay = factors(step * folded.astype(jnp.float32), wave_y)
+    edge_ref[0] = jnp.where(index == cell_count, 0.0, edge_x)
+    edge_ref[1] = 1.0 - self_part
+    edge_ref[2] = self_part
+    edge_ref[3] = mutual
+    edge_ref[4] = decay
+    edge_ref[5] = edge_y * edge_y
 
 
 def neighbours(values, decay):
@@ -246,7 +251,9 @@
 def respond(spectrum, coef, has_middle, middle):
     count = len(spectrum)
     unit_x, unit_y, keep, own, mutual, decay = coef[:6]
-    edge_x, edge_keep, edge_own, edge_mutual, edge_decay, keep_y, mutual_y = coef[6:]
+    edge_x, edge_keep, edge_own, edge_mutual, edge_decay, square_y, sign = coef[6:]
+    edge_keep, edge_own, edge_mutual = sign * edge_keep, sign * edge_own, sign * edge_mutual
+    keep_y, mutual_y = square_y * edge_keep, square_y * edge_mutual
     x = [s[0] for s in spectrum]
     y = [s[1] for s in spectrum]
     z = [s[2] for s in spectrum]
@@ -325,9 +332,12 @@
     ]
 
 
-def middle_kernel(rows_ref, coef_ref, twiddle_ref, forward_ref, back_ref, out_ref, work_ref, *, layers):
+def middle_kernel(
+    rows_ref, coef_ref, edge_ref, sign_ref, twiddle_ref, forward_ref, back_ref, out_ref, work_ref, *, layers
+):
     radix = twiddle_ref.shape[1]
     pieces = radix // 2
+    steps = rows_ref.shape[1] // sublanes
     items = layers * 3
     place = lax.broadcasted_iota(jnp.int32, (sublanes, lanes), 1)
     low = place < half
@@ -335,64 +345,67 @@
     forward = (forward_ref[0], forward_ref[1])
     back = (back_ref[0], back_ref[1])
 
-    def piece(plane, layer, part):
-        tile, upper = divmod(part, 2)
-        cut = slice(tile * lanes, (tile + 1) * lanes)
-        row = plane * layers + layer
-        first, second = rows_ref[row, :, cut], rows_ref[row + layers, :, cut]
-        if upper:
-            return jnp.where(low, pltpu.roll(first, half, 1), second)
-        return jnp.where(low, first, pltpu.roll(second, half, 1))
-
-    for item in range(items):
-        layer, c = divmod(item, 3)
-        z = [(piece(2 * p, layer, c), piece(2 * p, layer, 3 + c)) for p in range(pieces)]
-        for r, (real, imag) in enumerate(spread(z)):
-            if r > 0:
-                cosine, sine = twiddle_ref[0, r], twiddle_ref[1, r]
-                real, imag = real * cosine + imag * sine, imag * cosine - real * sine
-            start = item * sublanes
-            work_ref[r, start : start + sublanes, :lanes] = real
-            work_ref[r, start : start + sublanes, lanes:] = imag
-    for r in range(radix):
-        value = product(split(work_ref[r]), forward, dims)
-        spectrum = [
-            [
-                (
-                    value[(t * 3 + c) * sublanes : (t * 3 + c + 1) * sublanes, :lanes],
-                    value[(t * 3 + c) * sublanes : (t * 3 + c + 1) * sublanes, lanes:],
-                )
-                for c in range(3)
-            ]
-            for t in range(layers)
-        ]
-        coef = [coef_ref[n, r] for n in range(coef_count)]
-        out = respond(spectrum, coef, r == 0, place * radix + r == radix * half)
-        value = jnp.concatenate(
-            [jnp.concatenate([pair[0], pair[1]], axis=1) for layer in out for pair in layer]
-        )
-        work_ref[r] = product(split(value), back, dims)
-    for layer in range(layers):
-        parts = [[None] * 6 for _ in range(pieces)]
-        for c in range(3):
-            start = (layer * 3 + c) * sublanes
-            v = []
-            for r in range(radix):
-                real = work_ref[r, start : start + sublanes, :lanes]
-                imag = work_ref[r, start : start + sublanes, lanes:]
+    def run(step, carry):
+        here = pl.ds(pl.multiple_of(step * sublanes, sublanes), sublanes)
+
+        def piece(row, part):
+            tile, upper = divmod(part, 2)
+            cut = slice(tile * lanes, (tile + 1) * lanes)
+            first, second = rows_ref[row, here, cut], rows_ref[row + layers, here, cut]
+            if upper:
+                return jnp.where(low, pltpu.roll(first, half, 1), second)
+            return jnp.where(low, first, pltpu.roll(second, half, 1))
+
+        for item in range(items):
+            layer, c = divmod(item, 3)
+            rows = [2 * p * layers + layer for p in range(pieces)]
+            z = [(piece(row, c), piece(row, 3 + c)) for row in rows]
+            for r, (real, imag) in enumerate(spread(z)):
                 if r > 0:
                     cosine, sine = twiddle_ref[0, r], twiddle_ref[1, r]
-                    real, imag = real * cosine - imag * sine, imag * cosine + real * sine
-                v.append((real, imag))
-            for p, (real, imag) in enumerate(gather_back(v)):
-                parts[p][c], parts[p][3 + c] = real, imag
-        for p in range(pieces):
-            for tile in range(3):
-                first, second = parts[p][2 * tile], parts[p][2 * tile + 1]
-                cut = slice(tile * lanes, (tile + 1) * lanes)
+                    real, imag = real * cosine + imag * sine, imag * cosine - real * sine
+                start = item * sublanes
+                work_ref[r, start : start + sublanes, :lanes] = real
+                work_ref[r, start : start + sublanes, lanes:] = imag
+        for r in range(radix):
+            work_ref[r] = product(split(work_ref[r]), forward, dims)
+        for r in range(radix):
+            value = work_ref[r]
+            cuts = [slice(item * sublanes, (item + 1) * sublanes) for item in range(items)]
+            pairs = [(value[cut, :lanes], value[cut, lanes:]) for cut in cuts]
+            spectrum = [pairs[3 * t : 3 * t + 3] for t in range(layers)]
+            coef = [coef_ref[n, r, here] for n in range(coef_count)]
+            coef += [edge_ref[n, r : r + 1] for n in range(coef_count)] + [sign_ref[here]]
+            out = respond(spectrum, coef, r == 0, place * radix + r == radix * half)
+            work_ref[r] = jnp.concatenate(
+                [jnp.concatenate([pair[0], pair[1]], axis=1) for layer in out for pair in layer]
+            )
+        for r in range(radix):
+            work_ref[r] = product(split(work_ref[r]), back, dims)
+        for layer in range(layers):
+            parts = [[None] * 6 for _ in range(pieces)]
+            for c in range(3):
+                start = (layer * 3 + c) * sublanes
+                v = []
+                for r in range(radix):
+                    real = work_ref[r, start : start + sublanes, :lanes]
+                    imag = work_ref[r, start : start + sublanes, lanes:]
+                    if r > 0:
+                        cosine, sine = twiddle_ref[0, r], twiddle_ref[1, r]
+                        real, imag = real * cosine - imag * sine, imag * cosine + real * sine
+                    v.append((real, imag))
+                for p, (real, imag) in enumerate(gather_back(v)):
+                    parts[p][c], parts[p][3 + c] = real, imag
+            for p in range(pieces):
                 row = 2 * p * layers + layer
-                out_ref[row, :, cut] = jnp.where(low, first, pltpu.roll(second, half, 1))
-                out_ref[row + layers, :, cut] = jnp.where(low, pltpu.roll(first, half, 1), second)
+                for tile in range(3):
+                    first, second = parts[p][2 * tile], parts[p][2 * tile + 1]
+                    cut = slice(tile * lanes, (tile + 1) * lanes)
+                    out_ref[row, here, cut] = jnp.where(low, first, pltpu.roll(second, half, 1))
+                    out_ref[row + layers, here, cut] = jnp.where(low, pltpu.roll(first, half, 1), second)
+        return carry
+
+    lax.fori_loop(0, steps, run, 0)
 
 
 def exchange_kernel(link_ref, moment_ref, below_ref, above_ref, before_ref, after_ref, anisotropy_ref, out_ref):
@@ -414,7 +427,8 @@
 
 
 def last_kernel(
-    moment_ref, other_ref, edge_ref, back_ref, twiddle_ref, block_ref, field_ref, out_ref
+    moment_ref, other_ref, edge_ref, back_ref, twiddle_ref, block_ref, field_hbm, out_hbm,
+    field_ref, out_ref, field_sem, out_sem,
 ):
     rows = moment_ref.shape[1]
     turned = block_ref[...].T
@@ -442,14 +456,15 @@
         ],
         axis=1,
     )
+    for c in range(3):
+        field_ref[c] = other_ref[c] + demag[c * rows : (c + 1) * rows]
+    sends = [pltpu.make_async_copy(field_ref, field_hbm, field_sem)]
+    sends[0].start()
     span = rows // piece_count
     for n in range(piece_count):
         cut = pl.ds(n * span, span)
         m = [moment_ref[c, cut] for c in range(3)]
-        f = [other_ref[c, cut] + demag[c * rows + n * span : c * rows + (n + 1) * span] for c in range(3)]
-        for c in range(3):
-            field_ref[c, cut] = f[c]
-        first = cross(m, f)
+        first = cross(m, [field_ref[c, cut] for c in range(3)])
         second = cross(m, first)
         stepped = []
         for c in range(3):
@@ -458,6 +473,10 @@
         scale = lax.rsqrt(stepped[0] * stepped[0] + stepped[1] * stepped[1] + stepped[2] * stepped[2])
         for c in range(3):
             out_ref[c, cut] = stepped[c] * scale
+        sends.append(pltpu.make_async_copy(out_ref.at[:, cut], out_hbm.at[:, cut], out_sem.at[n]))
+        sends[-1].start()
+    for copy in sends:
+        copy.wait()
 
 
 def cross(first, second):
@@ -508,22 +527,28 @@
             pltpu.VMEM(side_shape, f32),
             pltpu.VMEM((cell_count, width), f32),
             dma((6,)),
-            dma((3,)),
+            dma((6,)),
         ],
         cost_estimate=pl.CostEstimate(flops=flops, bytes_accessed=4 << 20, transcendentals=0),
         name="first",
     )(polar[0], azimuth[0], saturation[0], edge, back, twiddle)
 
     base = (plane_index * layers + layer_index).astype(jnp.int32).reshape(1)
-    coefs = pl.pallas_call(
+    tables = (twiddle, forward, back)
+    *coefs, twiddle, forward, back = pl.pallas_call(
         functools.partial(coef_kernel, cell_count=cell_count),
-        out_shape=jax.ShapeDtypeStruct((coef_count, radix, slots, lanes), f32),
-        in_specs=[in_smem],
-        out_specs=in_vmem,
+        out_shape=[
+            jax.ShapeDtypeStruct((coef_count, radix, slots, lanes), f32),
+            jax.ShapeDtypeStruct((coef_count, radix, lanes), f32),
+            jax.ShapeDtypeStruct((slots, lanes), f32),
+        ]
+        + [jax.ShapeDtypeStruct(t.shape, t.dtype) for t in tables],
+        in_specs=[in_smem] + [in_vmem] * len(tables),
+        out_specs=[in_vmem] * (3 + len(tables)),
         compiler_params=small,
         cost_estimate=pl.CostEstimate(flops=20 << 20, bytes_accessed=1 << 20, transcendentals=1 << 16),
         name="coefs",
-    )(base)
+    )(base, *tables)
 
     below = shift(moment, "layer", 1)
     above = shift(moment, "layer", -1)
@@ -550,30 +575,30 @@
         lax.all_to_all, axis_name=both, split_axis=0, concat_axis=0, tiled=True
     )
     block = exchange_all(block.reshape(device_count, slots, width))
+    block, other = lax.optimization_barrier((block, other))
     block = pl.pallas_call(
         functools.partial(middle_kernel, layers=layers),
         out_shape=jax.ShapeDtypeStruct((device_count, slots, width), f32),
-        grid=(slots // sublanes,),
-        in_specs=[
-            pl.BlockSpec((device_count, sublanes, width), lambda g: (0, g, 0)),
-            pl.BlockSpec((coef_count, radix, sublanes, lanes), lambda g: (0, 0, g, 0)),
-            pl.BlockSpec(twiddle.shape, lambda g: (0, 0, 0, 0)),
-            pl.BlockSpec(forward.shape, lambda g: (0, 0, 0)),
-            pl.BlockSpec(back.shape, lambda g: (0, 0, 0)),
-        ],
-        out_specs=pl.BlockSpec((device_count, sublanes, width), lambda g: (0, g, 0)),
+        in_specs=[in_vmem] * 7,
+        out_specs=in_vmem,
         scratch_shapes=[pltpu.VMEM((radix, layers * 3 * sublanes, 2 * lanes), f32)],
         compiler_params=small,
         cost_estimate=pl.CostEstimate(flops=2000 << 20, bytes_accessed=4 << 20, transcendentals=0),
         name="middle",
-    )(block, coefs, twiddle, forward, back)
+    )(block, *coefs, twiddle, forward, back)
     block = exchange_all(block)
 
     field, stepped = pl.pallas_call(
         last_kernel,
         out_shape=[field_shape] * 2,
         in_specs=[in_vmem] * 6,
-        out_specs=[in_vmem] * 2,
+        out_specs=[in_any] * 2,
+        scratch_shapes=[
+            pltpu.VMEM((3, rows, cell_count), f32),
+            pltpu.VMEM((3, rows, cell_count), f32),
+            dma,
+            dma((piece_count,)),
+        ],
         compiler_params=small,
         cost_estimate=pl.CostEstimate(flops=flops, bytes_accessed=4 << 20, transcendentals=0),
         name="last",

time: 62.8 us -> 61.6 us (0.981)
  blocking collectives: 0 us -> 24.2 us
  waiting for transfers between devices: 27.3 us -> 6.74 us
  starting transfers between devices: 21.1 us -> 15.6 us
  local copies, waits for them, and re-layouts: 0.64 us -> 2.59 us
  Pallas kernels: 10.5 us -> 9.26 us
    all_to_all x0 -> x1, blocking collectives: none -> 24.2 us  [fast_body(): block = exchange_all(block)]
    all_to_all x1, waiting for transfers between devices: 20.3 us -> 6.3 us  [fast_body(): block = exchange_all(block.reshape(device_count, slots, width))]
    all_to_all x1 -> x0, waiting for transfers between devices: 6.96 us -> none  [fast_body(): block = exchange_all(block)]
    all_to_all x1 -> x0, starting transfers between devices: 3.63 us -> none  [fast_body(): block = exchange_all(block)]
    ppermute x4, starting transfers between devices: 10.2 us -> 8.29 us  [shift(): return lax.ppermute(value, axis, pairs)]
    unnamed x16 -> x20, local copies, waits for them, and re-layouts: 0.04 us -> 1.33 us
    pallas_call x1, Pallas kernels: 4.14 us -> 3.3 us  [fast_body(): pl.pallas_call(functools.partial(middle_kernel, layers=layers), out_shape...]
  transfers between devices with their start and end apart: 6 -> 5, of which waited for: 2 -> 2; matrix products, arithmetic and copies ran while one was open for 3% -> 4% of each run, Pallas kernels for 2% -> 2%
where the time goes in v2:
time: 61.6 us; the launch traced here: 61.3 us
  blocking collectives  24.2 us (39%)
  starting transfers between devices  15.6 us (25%)
  Pallas kernels  9.26 us (15%)
  waiting for transfers between devices  6.74 us (11%)
  local copies, waits for them, and re-layouts  2.59 us (4%)
  between operations  1.46 us (2%)
  other arithmetic  1.34 us (2%)
    all_to_all x1, blocking collectives, fast_body(): block = exchange_all(block)  24.2 us
    ppermute x4, starting transfers between devices, shift(): return lax.ppermute(value, axis, pairs)  8.29 us
    all_to_all x1, starting transfers between devices, fast_body(): block = exchange_all(block.reshape(device_count, slots, width))  7.33 us
    all_to_all x1, waiting for transfers between devices, fast_body(): block = exchange_all(block.reshape(device_count, slots, width))  6.3 us
    pallas_call x1, Pallas kernels, fast_body(): pl.pallas_call(functools.partial(middle_kernel, layers=layers), out_shape...  3.3 us
    pallas_call x1, Pallas kernels, fast_body(): pl.pallas_call(first_kernel, out_shape=[field_shape, jax.ShapeDtypeStruct...  3.25 us
    pallas_call x1, Pallas kernels, fast_body(): pl.pallas_call(last_kernel, out_shape=[field_shape] * 2, in_specs=[in_vme...  1.65 us
    another operation x1, other arithmetic, fast_body(): jnp.stack([stiffness[0], coupling[jnp.maximum(layer_index - 1, 0)], coupl...  1.34 us
  transfers between devices with their start and end apart: 5, of which 2 were waited for; matrix products, arithmetic and copies ran while one was open for 4% of the time, Pallas kernels for 2%

profile of v2, /device:TPU:0, one launch (start us, length us, event | category | flops | bytes accessed | tf_op | source)
XLA Modules:
  0.0 61.3 jit_solution(4599118991858366797)
XLA Ops:
  0.6 3.2 %first.1 = (f32[3,64,512]{2,1,0:T(8,128)}, f32[2,8,512]{2,1,0:T(8,128)}, f32[512,384]{1,0:T(8,128)}) custom-call(f32[64,512]{1,0:T(8,128)} %bitcast.16, f32[64,512]{1,0:T(8,128)} %bitcast.17, f32[64,512]{1,0:T(8,128)} %bitcast.18, bf16[2,256,256]{2,1,0:T(8,128)(2,1)} %constant.28.clone.edge_hbm.edge_ref, ...), custom_call_target="tpu_custom_call" | custom-call | flops 1207959552 | bytes 4194304 | tf_op jit(solution)/shard_map/first/pallas_call | solution.py:516
  3.9 0.0 copy-start
  3.9 0.0 copy-start.8
  3.9 0.0 copy-start.1
  3.9 0.0 copy-start.2
  3.9 7.3 %all-to-all-start = ((f32[32,16,384]{2,1,0:T(8,128)}), f32[32,16,384]{2,1,0:T(8,128)S(1)}, u32[]{:S(2)}, u32[]{:S(2)}) async-start(f32[32,16,384]{2,1,0:T(8,128)} %bitcast.15), calls=%async_computation | async-start | bytes 1572864 | tf_op jit(solution)/shard_map/all_to_all | solution.py:577
  11.3 0.0 copy-start.4
  11.3 2.2 %collective-permute-start = (f32[3,64,512]{2,1,0:T(8,128)S(1)}, f32[3,64,512]{2,1,0:T(8,128)S(1)}, u32[]{:S(2)}, u32[]{:S(2)}) collective-permute-start(f32[3,64,512]{2,1,0:T(8,128)S(1)} %copy-done), channel_id=1, source_target_pairs={{0,8},{8,16},{16,24},{1,9},{9,17},{17,25},{2,10},{10,18},{18,26},{... | collective-permute-start | bytes 1179656 | tf_op jit(solution)/shard_map/ppermute | solution.py:493
  13.5 1.3 %collective-permute-start.1 = (f32[3,64,512]{2,1,0:T(8,128)S(1)}, f32[3,64,512]{2,1,0:T(8,128)S(1)}, u32[]{:S(2)}, u32[]{:S(2)}) collective-permute-start(f32[3,64,512]{2,1,0:T(8,128)S(1)} %copy-done), channel_id=1, source_target_pairs={{8,0},{16,8},{24,16},{9,1},{17,9},{25,17},{10,2},{18,10},{26,18},{... | collective-permute-start | bytes 1179656 | tf_op jit(solution)/shard_map/ppermute | solution.py:493
  14.8 0.6 slice_bitcast_fusion
  15.4 3.5 %collective-permute-start.2 = (f32[8,512]{1,0:T(8,128)}, f32[8,512]{1,0:T(8,128)S(1)}, u32[]{:S(2)}, u32[]{:S(2)}) collective-permute-start(f32[8,512]{1,0:T(8,128)} %get-tuple-element.29), channel_id=1, source_target_pairs={{0,1},{1,2},{2,3},{3,4},{4,5},{5,6},{6,7},{8,9},{9,10},{10,11},{11... | collective-permute-start | bytes 49160 | tf_op jit(solution)/shard_map/ppermute | solution.py:493
  18.9 1.3 %collective-permute-start.3 = (f32[8,512]{1,0:T(8,128)}, f32[8,512]{1,0:T(8,128)S(1)}, u32[]{:S(2)}, u32[]{:S(2)}) collective-permute-start(f32[8,512]{1,0:T(8,128)} %get-tuple-element.28), channel_id=1, source_target_pairs={{1,0},{2,1},{3,2},{4,3},{5,4},{6,5},{7,6},{9,8},{10,9},{11,10},{12... | collective-permute-start | bytes 49160 | tf_op jit(solution)/shard_map/ppermute | solution.py:493
  20.9 0.0 copy-start.9
  20.9 0.6 %copy-done.9 = f32[3]{0:T(128)S(1)} copy-done((f32[3]{0:T(128)S(1)}, f32[3]{0:T(128)}, u32[]{:S(2)}) %copy-start.9) | copy-done | bytes 36
  21.6 0.6 %fusion = (f32[1]{0:T(128)}, f32[1]{0:T(128)}) fusion(f32[3]{0:T(128)S(1)} %copy-done.9, s32[]{:T(128)S(6)} %max.3, s32[]{:T(128)S(6)} %select_n.4), kind=kLoop, calls=%fused_computation.3 | loop fusion | bytes 24 | tf_op jit(solution)/shard_map/dynamic_slice | solution.py:560
  22.2 1.3 %pad_maximum_fusion.link_ref = f32[3]{0:T(128)S(1)} fusion(f32[1]{0:T(128)} %get-tuple-element.31, f32[1]{0:T(128)} %get-tuple-element.30, f32[1]{0:T(128)S(6)} %copy.12), kind=kLoop, calls=%fused_computation.2 | loop fusion | flops 6 | bytes 24 | tf_op jit(solution)/shard_map/stack | solution.py:557
  23.5 0.0 copy-done.1
  23.6 0.0 copy-start.3
  23.6 0.2 coefs.1
  23.8 0.0 copy-start.5
  23.8 0.6 %copy-done.5 = f32[2,8,8,128]{3,2,1,0:T(8,128)} copy-done((f32[2,8,8,128]{3,2,1,0:T(8,128)}, f32[2,8,8,128]{3,2,1,0:T(8,128)S(1)}, u32[]{:S(2)}) %copy-start.5) | copy-done | bytes 65560
  24.4 0.0 collective-permute-done.2.before_ref
  24.4 0.4 collective-permute-done.3.after_ref
  24.8 0.0 collective-permute-done.below_ref
  24.8 0.0 collective-permute-done.1.above_ref
  24.8 0.0 copy-start.6
  24.9 0.9 %exchange.1.other_ref = f32[3,64,512]{2,1,0:T(8,128)S(1)} custom-call(f32[3]{0:T(128)S(1)} %pad_maximum_fusion.link_ref, f32[3,64,512]{2,1,0:T(8,128)S(1)} %copy-done, f32[3,64,512]{2,1,0:T(8,128)S(1)} %collective-permute-done.below_ref, f32[3,64,512]{2,1,0:T(8,128)S(1)} %collective-permute-done.1.above_ref, f32[8,512]{1,0:T(8,128)S(1)} %collective-permute-done.2.before_ref, ...), custom_call_target="tpu_custom_call" | custom-call | flops 20971520 | bytes 2097152 | tf_op jit(solution)/shard_map/exchange/pallas_call | solution.py:564
  25.7 6.3 %all-to-all-done.rows_ref = f32[32,16,384]{2,1,0:T(8,128)S(1)} async-done(((f32[32,16,384]{2,1,0:T(8,128)}), f32[32,16,384]{2,1,0:T(8,128)S(1)}, u32[]{:S(2)}, u32[]{:S(2)}) %all-to-all-start) | async-done | bytes 786464 | tf_op jit(solution)/shard_map/all_to_all | solution.py:577
  32.0 3.3 %middle.1 = f32[32,16,384]{2,1,0:T(8,128)S(1)} custom-call(f32[32,16,384]{2,1,0:T(8,128)S(1)} %all-to-all-done.rows_ref, f32[6,8,16,128]{3,2,1,0:T(8,128)S(1)} %get-tuple-element.22.coef_ref, f32[6,8,128]{2,1,0:T(8,128)S(1)} %get-tuple-element.23.edge_ref, f32[16,128]{1,0:T(8,128)S(1)} %get-tuple-element.24.sign_ref, f32[2,8,8,128]{3,2,1,0:T(8,128)S(1)} %copy-done.6, ...), custom_call_target="tpu_custom_call" | custom-call | flops 2097152000 | bytes 4194304 | tf_op jit(solution)/shard_map/middle/pallas_call | solution.py:579
  35.3 0.0 copy-start.7
  35.4 24.2 %all_to_all.10 = f32[32,16,384]{2,1,0:T(8,128)S(1)} all-to-all(f32[32,16,384]{2,1,0:T(8,128)S(1)} %middle.1), channel_id=1, replica_groups=mesh['layer'=4,'plane'=8] {'plane','layer'}, dimensions={0} | all-to-all | bytes 1572864 | tf_op jit(solution)/shard_map/all_to_all | solution.py:589
  59.6 1.7 %last.1 = (f32[3,64,512]{2,1,0:T(8,128)}, f32[3,64,512]{2,1,0:T(8,128)}) custom-call(f32[3,64,512]{2,1,0:T(8,128)S(1)} %copy-done, f32[3,64,512]{2,1,0:T(8,128)S(1)} %exchange.1.other_ref, bf16[2,256,256]{2,1,0:T(8,128)(2,1)S(1)} %copy-done.7, bf16[2,256,256]{2,1,0:T(8,128)(2,1)S(1)} %get-tuple-element.19.back_ref, f32[2,8,8,128]{3,2,1,0:T(8,128)S(1)} %copy-done.6, ...), custom_call_target="tpu_custom_call" | custom-call | flops 1207959552 | bytes 4194304 | tf_op jit(solution)/shard_map/last/pallas_call | solution.py:591
  (7 shorter events, 0.0 us)
Async XLA Ops:
  3.9 7.4 %copy-start = (f32[3,64,512]{2,1,0:T(8,128)S(1)}, f32[3,64,512]{2,1,0:T(8,128)}, u32[]{:S(2)}) copy-start(f32[3,64,512]{2,1,0:T(8,128)} %get-tuple-element.15.moment_ref) | copy-start | bytes 1179652
  3.9 10.9 %copy-start.8 = (f32[2,8,512]{2,1,0:T(8,128)S(1)}, f32[2,8,512]{2,1,0:T(8,128)}, u32[]{:S(2)}) copy-start(f32[2,8,512]{2,1,0:T(8,128)} %get-tuple-element.17) | copy-start | bytes 98308
  3.9 19.6 %copy-start.1 = (bf16[2,256,256]{2,1,0:T(8,128)(2,1)S(1)}, bf16[2,256,256]{2,1,0:T(8,128)(2,1)}, u32[]{:S(2)}) copy-start(bf16[2,256,256]{2,1,0:T(8,128)(2,1)} %constant.30.clone.back_hbm.refs_2_) | copy-start | bytes 786436
  3.9 19.6 %copy-start.2 = (bf16[2,256,256]{2,1,0:T(8,128)(2,1)S(1)}, bf16[2,256,256]{2,1,0:T(8,128)(2,1)}, u32[]{:S(2)}) copy-start(bf16[2,256,256]{2,1,0:T(8,128)(2,1)} %constant.29.clone.refs_1_) | copy-start | bytes 786436
  3.9 28.1 %all-to-all-start = ((f32[32,16,384]{2,1,0:T(8,128)}), f32[32,16,384]{2,1,0:T(8,128)S(1)}, u32[]{:S(2)}, u32[]{:S(2)}) async-start(f32[32,16,384]{2,1,0:T(8,128)} %bitcast.15), calls=%async_computation | async-start | bytes 1572864 | tf_op jit(solution)/shard_map/all_to_all | solution.py:577
  11.3 12.3 %copy-start.4 = (f32[2,8,8,128]{3,2,1,0:T(8,128)S(1)}, f32[2,8,8,128]{3,2,1,0:T(8,128)}, u32[]{:S(2)}) copy-start(f32[2,8,8,128]{3,2,1,0:T(8,128)} %constant.31.clone.twiddle_hbm.refs_0_) | copy-start | bytes 196612
  11.3 13.5 %collective-permute-start = (f32[3,64,512]{2,1,0:T(8,128)S(1)}, f32[3,64,512]{2,1,0:T(8,128)S(1)}, u32[]{:S(2)}, u32[]{:S(2)}) collective-permute-start(f32[3,64,512]{2,1,0:T(8,128)S(1)} %copy-done), channel_id=1, source_target_pairs={{0,8},{8,16},{16,24},{1,9},{9,17},{17,25},{2,10},{10,18},{18,26},{... | collective-permute-start | bytes 1179656 | tf_op jit(solution)/shard_map/ppermute | solution.py:493
  13.5 11.4 %collective-permute-start.1 = (f32[3,64,512]{2,1,0:T(8,128)S(1)}, f32[3,64,512]{2,1,0:T(8,128)S(1)}, u32[]{:S(2)}, u32[]{:S(2)}) collective-permute-start(f32[3,64,512]{2,1,0:T(8,128)S(1)} %copy-done), channel_id=1, source_target_pairs={{8,0},{16,8},{24,16},{9,1},{17,9},{25,17},{10,2},{18,10},{26,18},{... | collective-permute-start | bytes 1179656 | tf_op jit(solution)/shard_map/ppermute | solution.py:493
  15.4 9.0 %collective-permute-start.2 = (f32[8,512]{1,0:T(8,128)}, f32[8,512]{1,0:T(8,128)S(1)}, u32[]{:S(2)}, u32[]{:S(2)}) collective-permute-start(f32[8,512]{1,0:T(8,128)} %get-tuple-element.29), channel_id=1, source_target_pairs={{0,1},{1,2},{2,3},{3,4},{4,5},{5,6},{6,7},{8,9},{9,10},{10,11},{11... | collective-permute-start | bytes 49160 | tf_op jit(solution)/shard_map/ppermute | solution.py:493
  18.9 5.9 %collective-permute-start.3 = (f32[8,512]{1,0:T(8,128)}, f32[8,512]{1,0:T(8,128)S(1)}, u32[]{:S(2)}, u32[]{:S(2)}) collective-permute-start(f32[8,512]{1,0:T(8,128)} %get-tuple-element.28), channel_id=1, source_target_pairs={{1,0},{2,1},{3,2},{4,3},{5,4},{6,5},{7,6},{9,8},{10,9},{11,10},{12... | collective-permute-start | bytes 49160 | tf_op jit(solution)/shard_map/ppermute | solution.py:493
  20.9 0.7 %copy-start.9 = (f32[3]{0:T(128)S(1)}, f32[3]{0:T(128)}, u32[]{:S(2)}) copy-start(f32[3]{0:T(128)} %param.15) | copy-start | bytes 40
  23.6 1.3 %copy-start.3 = (f32[1,64,512]{2,1,0:T(8,128)S(1)}, f32[1,64,512]{2,1,0:T(8,128)}, u32[]{:S(2)}) copy-start(f32[1,64,512]{2,1,0:T(8,128)} %param.13) | copy-start | bytes 393220
  23.8 0.6 %copy-start.5 = (f32[2,8,8,128]{3,2,1,0:T(8,128)}, f32[2,8,8,128]{3,2,1,0:T(8,128)S(1)}, u32[]{:S(2)}) copy-start(f32[2,8,8,128]{3,2,1,0:T(8,128)S(1)} %get-tuple-element.20.twiddle_ref) | copy-start | bytes 196612
  24.8 7.2 %copy-start.6 = (f32[2,8,8,128]{3,2,1,0:T(8,128)S(1)}, f32[2,8,8,128]{3,2,1,0:T(8,128)}, u32[]{:S(2)}) copy-start(f32[2,8,8,128]{3,2,1,0:T(8,128)} %copy-done.5) | copy-start | bytes 196612
  35.3 24.3 %copy-start.7 = (bf16[2,256,256]{2,1,0:T(8,128)(2,1)S(1)}, bf16[2,256,256]{2,1,0:T(8,128)(2,1)}, u32[]{:S(2)}) copy-start(bf16[2,256,256]{2,1,0:T(8,128)(2,1)} %constant.28.clone.edge_hbm.edge_ref) | copy-start | bytes 786436

commit v3 on v2

--- a/solution.py
+++ b/solution.py
@@ -8,6 +8,7 @@
 from jax.experimental import pallas as pl
 from jax.experimental.pallas import tpu as pltpu
 from jax.sharding import PartitionSpec as P
+
 
 side_length = 512.0
 spacing = 1.2
@@ -42,11 +43,11 @@
     return split_table(np.concatenate([rows[0], -rows[1]]))
 
 
-def short_tables():
+def short_table():
     turns = np.outer(np.arange(lanes), np.arange(lanes)) % lanes
     phase = turns * (2.0 * np.pi / lanes)
     c, s = np.cos(phase), np.sin(phase)
-    return split_table(np.block([[c, -s], [s, c]])), split_table(np.block([[c, s], [-s, c]]))
+    return split_table(np.block([[c, s], [-s, c]]))
 
 
 def twiddle_table(radix):
@@ -85,7 +86,7 @@
     polar_hbm, azimuth_hbm, saturation_hbm, edge_hbm, back_hbm, twiddle_hbm, moment_hbm, side_hbm, out_hbm,
     angle_ref, edge_ref, back_ref, twiddle_ref, moment_ref, side_ref, rows_ref, in_sem, out_sem,
 ):
-    rows, cell_count = angle_ref.shape[1:]
+    rows, _ = angle_ref.shape[1:]
     sources = (polar_hbm, azimuth_hbm, saturation_hbm, edge_hbm, back_hbm, twiddle_hbm)
     places = (angle_ref.at[0], angle_ref.at[1], angle_ref.at[2], edge_ref, back_ref, twiddle_ref)
     loads = [
@@ -333,7 +334,7 @@
 
 
 def middle_kernel(
-    rows_ref, coef_ref, edge_ref, sign_ref, twiddle_ref, forward_ref, back_ref, out_ref, work_ref, *, layers
+    rows_ref, coef_ref, edge_ref, sign_ref, twiddle_ref, back_ref, out_ref, work_ref, *, layers
 ):
     radix = twiddle_ref.shape[1]
     pieces = radix // 2
@@ -342,8 +343,10 @@
     place = lax.broadcasted_iota(jnp.int32, (sublanes, lanes), 1)
     low = place < half
     dims = ((1,), (0,))
-    forward = (forward_ref[0], forward_ref[1])
     back = (back_ref[0], back_ref[1])
+    upper = [jnp.concatenate([b[:lanes, :lanes], b[lanes:, :lanes]], axis=1) for b in back]
+    lower = [jnp.concatenate([b[:lanes, lanes:], b[lanes:, lanes:]], axis=1) for b in back]
+    forward = tuple(jnp.concatenate(pair) for pair in zip(upper, lower))
 
     def run(step, carry):
         here = pl.ds(pl.multiple_of(step * sublanes, sublanes), sublanes)
@@ -408,15 +411,18 @@
     lax.fori_loop(0, steps, run, 0)
 
 
-def exchange_kernel(link_ref, moment_ref, below_ref, above_ref, before_ref, after_ref, anisotropy_ref, out_ref):
+def exchange_kernel(place_ref, stiffness_ref, coupling_ref, moment_ref, below_ref, above_ref, anisotropy_ref, out_ref, scale_ref):
+    scale_ref[...] = jnp.full_like(scale_ref, stiffness_ref[0])
     rows, cell_count = anisotropy_ref.shape
     row = lax.broadcasted_iota(jnp.int32, (rows, cell_count), 0)
     column = lax.broadcasted_iota(jnp.int32, (rows, cell_count), 1)
-    stiffness, lower_link, upper_link = link_ref[0], link_ref[1], link_ref[2]
+    stiffness = stiffness_ref[0]
+    lower_link = coupling_ref[jnp.maximum(place_ref[1] - 1, 0)]
+    upper_link = coupling_ref[jnp.minimum(place_ref[1], coupling_ref.shape[0] - 1)]
     for c in range(3):
         m = moment_ref[c]
-        before = jnp.where(row == 0, before_ref[c : c + 1], pltpu.roll(m, 1, 0))
-        after = jnp.where(row == rows - 1, after_ref[c : c + 1], pltpu.roll(m, rows - 1, 0))
+        before = jnp.where(row == 0, 0.0, pltpu.roll(m, 1, 0))
+        after = jnp.where(row == rows - 1, 0.0, pltpu.roll(m, rows - 1, 0))
         left = jnp.where(column == 0, 0.0, pltpu.roll(m, 1, 1))
         right = jnp.where(column == cell_count - 1, 0.0, pltpu.roll(m, cell_count - 1, 1))
         total = stiffness * (before + after + left + right)
@@ -427,10 +433,16 @@
 
 
 def last_kernel(
-    moment_ref, other_ref, edge_ref, back_ref, twiddle_ref, block_ref, field_hbm, out_hbm,
-    field_ref, out_ref, field_sem, out_sem,
+    before_any, after_any, scale_any, moment_ref, other_ref, edge_ref, back_ref, twiddle_ref, block_ref,
+    field_hbm, out_hbm, field_ref, out_ref, side_ref, field_sem, out_sem, side_sem,
 ):
     rows = moment_ref.shape[1]
+    sides = [
+        pltpu.make_async_copy(source, side_ref.at[n], side_sem.at[n])
+        for n, source in enumerate((before_any, after_any, scale_any))
+    ]
+    for copy in sides:
+        copy.start()
     turned = block_ref[...].T
     dims = ((1,), (0,))
     waves = []
@@ -456,8 +468,12 @@
         ],
         axis=1,
     )
+    for copy in sides:
+        copy.wait()
     for c in range(3):
         field_ref[c] = other_ref[c] + demag[c * rows : (c + 1) * rows]
+        field_ref[c, :1] += side_ref[2, :1] * side_ref[0, c : c + 1]
+        field_ref[c, rows - 1 :] += side_ref[2, :1] * side_ref[1, c : c + 1]
     sends = [pltpu.make_async_copy(field_ref, field_hbm, field_sem)]
     sends[0].start()
     span = rows // piece_count
@@ -504,7 +520,7 @@
     width = 6 * rows
     f32, bf16 = jnp.float32, jnp.bfloat16
     edge = jnp.asarray(edge_table())
-    forward, back = (jnp.asarray(t) for t in short_tables())
+    back = jnp.asarray(short_table())
     twiddle = jnp.asarray(twiddle_table(radix))
     field_shape = jax.ShapeDtypeStruct((3, rows, cell_count), f32)
     side_shape = (2, sublanes, cell_count)
@@ -533,9 +549,9 @@
         name="first",
     )(polar[0], azimuth[0], saturation[0], edge, back, twiddle)
 
-    base = (plane_index * layers + layer_index).astype(jnp.int32).reshape(1)
-    tables = (twiddle, forward, back)
-    *coefs, twiddle, forward, back = pl.pallas_call(
+    base = jnp.stack([plane_index * layers + layer_index, layer_index]).astype(jnp.int32)
+    tables = (twiddle, back)
+    *coefs, kept_twiddle, kept_back = pl.pallas_call(
         functools.partial(coef_kernel, cell_count=cell_count),
         out_shape=[
             jax.ShapeDtypeStruct((coef_count, radix, slots, lanes), f32),
@@ -554,22 +570,15 @@
     above = shift(moment, "layer", -1)
     before = shift(side[1], "plane", 1)
     after = shift(side[0], "plane", -1)
-    links = jnp.stack(
-        [
-            stiffness[0],
-            coupling[jnp.maximum(layer_index - 1, 0)],
-            coupling[jnp.minimum(layer_index, coupling.shape[0] - 1)],
-        ]
-    )
-    other = pl.pallas_call(
+    other, scale = pl.pallas_call(
         exchange_kernel,
-        out_shape=field_shape,
-        in_specs=[in_smem] + [in_vmem] * 6,
-        out_specs=in_vmem,
+        out_shape=[field_shape, jax.ShapeDtypeStruct(side_shape[1:], f32)],
+        in_specs=[in_smem] * 3 + [in_vmem] * 4,
+        out_specs=[in_vmem] * 2,
         compiler_params=small,
         cost_estimate=pl.CostEstimate(flops=20 << 20, bytes_accessed=2 << 20, transcendentals=0),
         name="exchange",
-    )(links, moment, below, above, before, after, anisotropy[0])
+    )(base, stiffness, coupling, moment, below, above, anisotropy[0])
 
     exchange_all = functools.partial(
         lax.all_to_all, axis_name=both, split_axis=0, concat_axis=0, tiled=True
@@ -579,30 +588,33 @@
     block = pl.pallas_call(
         functools.partial(middle_kernel, layers=layers),
         out_shape=jax.ShapeDtypeStruct((device_count, slots, width), f32),
-        in_specs=[in_vmem] * 7,
+        in_specs=[in_vmem] * 6,
         out_specs=in_vmem,
         scratch_shapes=[pltpu.VMEM((radix, layers * 3 * sublanes, 2 * lanes), f32)],
         compiler_params=small,
         cost_estimate=pl.CostEstimate(flops=2000 << 20, bytes_accessed=4 << 20, transcendentals=0),
         name="middle",
-    )(block, *coefs, twiddle, forward, back)
+    )(block, *coefs, kept_twiddle, kept_back)
+    block, before, after = lax.optimization_barrier((block, before, after))
     block = exchange_all(block)
 
     field, stepped = pl.pallas_call(
         last_kernel,
         out_shape=[field_shape] * 2,
-        in_specs=[in_vmem] * 6,
+        in_specs=[in_any] * 3 + [in_vmem] * 6,
         out_specs=[in_any] * 2,
         scratch_shapes=[
             pltpu.VMEM((3, rows, cell_count), f32),
             pltpu.VMEM((3, rows, cell_count), f32),
+            pltpu.VMEM((3, *side_shape[1:]), f32),
             dma,
             dma((piece_count,)),
+            dma((3,)),
         ],
         compiler_params=small,
         cost_estimate=pl.CostEstimate(flops=flops, bytes_accessed=4 << 20, transcendentals=0),
         name="last",
-    )(moment, other, edge, back, twiddle, block.reshape(cell_count, width))
+    )(before, after, scale, moment, other, edge, back, twiddle, block.reshape(cell_count, width))
     return field[None], stepped[None]
 
 

time: 61.6 us -> 61.3 us (level)
  waiting for transfers between devices: 6.74 us -> 9.37 us
  local copies, waits for them, and re-layouts: 2.59 us -> 0.68 us
  other arithmetic: 1.34 us -> 0.08 us
    all_to_all x1, waiting for transfers between devices: 6.3 us -> 9.36 us  [fast_body(): block = exchange_all(block.reshape(device_count, slots, width))]
    another operation x1, other arithmetic: 1.34 us -> 0.08 us  [fast_body(): jnp.stack([plane_index * layers + layer_index, layer_index])]
    unnamed x20 -> x14, local copies, waits for them, and re-layouts: 1.33 us -> 0.68 us
    dynamic_slice x1 -> x0, local copies, waits for them, and re-layouts: 0.65 us -> none  [fast_body(): coupling[jnp.maximum(layer_index - 1, 0)]]
  transfers between devices with their start and end apart: 5 -> 5, of which waited for: 2 -> 1; matrix products, arithmetic and copies ran while one was open for 4% -> 0% of each run, Pallas kernels for 2% -> 8%
where the time goes in v3:
time: 61.3 us; the launch traced here: 61 us
  blocking collectives  23.9 us (39%)
  starting transfers between devices  15.6 us (25%)
  Pallas kernels  9.86 us (16%)
  waiting for transfers between devices  9.37 us (15%)
  between operations  1.46 us (2%)
  local copies, waits for them, and re-layouts  0.68 us (1%)
    all_to_all x1, blocking collectives, fast_body(): block = exchange_all(block)  23.9 us
    all_to_all x1, waiting for transfers between devices, fast_body(): block = exchange_all(block.reshape(device_count, slots, width))  9.36 us
    ppermute x4, starting transfers between devices, shift(): return lax.ppermute(value, axis, pairs)  8.3 us
    all_to_all x1, starting transfers between devices, fast_body(): block = exchange_all(block.reshape(device_count, slots, width))  7.33 us
    pallas_call x1, Pallas kernels, fast_body(): pl.pallas_call(functools.partial(middle_kernel, layers=layers), out_shape...  3.26 us
    pallas_call x1, Pallas kernels, fast_body(): pl.pallas_call(first_kernel, out_shape=[field_shape, jax.ShapeDtypeStruct...  3.23 us
    pallas_call x1, Pallas kernels, fast_body(): pl.pallas_call(last_kernel, out_shape=[field_shape] * 2, in_specs=[in_any...  1.77 us
  transfers between devices with their start and end apart: 5, of which 1 were waited for; matrix products, arithmetic and copies ran while one was open for 0% of the time, Pallas kernels for 8%

profile of v3, /device:TPU:0, one launch (start us, length us, event | category | flops | bytes accessed | tf_op | source)
XLA Modules:
  0.0 61.0 jit_solution(11081828395312291054)
XLA Ops:
  0.6 3.2 %first.1 = (f32[3,64,512]{2,1,0:T(8,128)}, f32[2,8,512]{2,1,0:T(8,128)}, f32[512,384]{1,0:T(8,128)}) custom-call(f32[64,512]{1,0:T(8,128)} %bitcast.17, f32[64,512]{1,0:T(8,128)} %bitcast.18, f32[64,512]{1,0:T(8,128)} %bitcast.19, bf16[2,256,256]{2,1,0:T(8,128)(2,1)} %constant.16.clone.edge_hbm.edge_ref, ...), custom_call_target="tpu_custom_call" | custom-call | flops 1207959552 | bytes 4194304 | tf_op jit(solution)/shard_map/first/pallas_call | solution.py:532
  3.9 0.0 copy-start
  3.9 0.0 copy-start.6
  3.9 0.0 copy-start.1
  3.9 7.3 %all-to-all-start = ((f32[32,16,384]{2,1,0:T(8,128)}), f32[32,16,384]{2,1,0:T(8,128)S(1)}, u32[]{:S(2)}, u32[]{:S(2)}) async-start(f32[32,16,384]{2,1,0:T(8,128)} %bitcast.16), calls=%async_computation | async-start | bytes 1572864 | tf_op jit(solution)/shard_map/all_to_all | solution.py:586
  11.2 0.0 copy-start.3
  11.3 0.0 copy-done
  11.3 2.2 %collective-permute-start = (f32[3,64,512]{2,1,0:T(8,128)S(1)}, f32[3,64,512]{2,1,0:T(8,128)S(1)}, u32[]{:S(2)}, u32[]{:S(2)}) collective-permute-start(f32[3,64,512]{2,1,0:T(8,128)S(1)} %copy-done), channel_id=1, source_target_pairs={{0,8},{8,16},{16,24},{1,9},{9,17},{17,25},{2,10},{10,18},{18,26},{... | collective-permute-start | bytes 1179656 | tf_op jit(solution)/shard_map/ppermute | solution.py:509
  13.5 1.3 %collective-permute-start.1 = (f32[3,64,512]{2,1,0:T(8,128)S(1)}, f32[3,64,512]{2,1,0:T(8,128)S(1)}, u32[]{:S(2)}, u32[]{:S(2)}) collective-permute-start(f32[3,64,512]{2,1,0:T(8,128)S(1)} %copy-done), channel_id=1, source_target_pairs={{8,0},{16,8},{24,16},{9,1},{17,9},{25,17},{10,2},{18,10},{26,18},{... | collective-permute-start | bytes 1179656 | tf_op jit(solution)/shard_map/ppermute | solution.py:509
  14.8 0.0 copy-done.6
  14.8 3.5 %collective-permute-start.2 = (f32[8,512]{1,0:T(8,128)S(1)}, f32[8,512]{1,0:T(8,128)S(1)}, u32[]{:S(2)}, u32[]{:S(2)}) collective-permute-start(f32[8,512]{1,0:T(8,128)S(1)} %get-tuple-element.37), channel_id=1, source_target_pairs={{0,1},{1,2},{2,3},{3,4},{4,5},{5,6},{6,7},{8,9},{9,10},{10,11},{11... | collective-permute-start | bytes 49160 | tf_op jit(solution)/shard_map/ppermute | solution.py:509
  18.3 1.3 %collective-permute-start.3 = (f32[8,512]{1,0:T(8,128)S(1)}, f32[8,512]{1,0:T(8,128)S(1)}, u32[]{:S(2)}, u32[]{:S(2)}) collective-permute-start(f32[8,512]{1,0:T(8,128)S(1)} %get-tuple-element.36), channel_id=1, source_target_pairs={{1,0},{2,1},{3,2},{4,3},{5,4},{6,5},{7,6},{9,8},{10,9},{11,10},{12... | collective-permute-start | bytes 49160 | tf_op jit(solution)/shard_map/ppermute | solution.py:509
  20.3 0.1 pad_add_fusion.place_ref.base_ref
  20.4 0.0 copy-done.1
  20.4 0.0 copy-done.3
  20.4 0.0 copy-start.2
  20.4 0.7 %coefs.1 = (f32[6,8,16,128]{3,2,1,0:T(8,128)S(1)}, f32[6,8,128]{2,1,0:T(8,128)S(1)}, f32[16,128]{1,0:T(8,128)S(1)}, f32[2,8,8,128]{3,2,1,0:T(8,128)S(1)}, bf16[2,256,256]{2,1,0:T(8,128)(2,1)S(1)}) custom-call(s32[2]{0:T(128)S(1)} %pad_add_fusion.place_ref.base_ref, f32[2,8,8,128]{3,2,1,0:T(8,128)S(1)} %copy-done.3, bf16[2,256,256]{2,1,0:T(8,128)(2,1)S(1)} %copy-done.1), custom_call_target="tpu_custom_call" | custom-call | flops 20971520 | bytes 1048576 | tf_op jit(solution)/shard_map/coefs/pallas_call | solution.py:554
  21.1 0.0 copy-start.4
  21.1 0.0 collective-permute-done.below_ref
  21.1 0.0 collective-permute-done.1.above_ref
  21.1 0.1 copy-done.2
  21.3 0.5 copy-done.4
  21.8 0.9 %exchange.1 = (f32[3,64,512]{2,1,0:T(8,128)S(1)}, f32[8,512]{1,0:T(8,128)S(1)}) custom-call(s32[2]{0:T(128)S(1)} %pad_add_fusion.place_ref.base_ref, f32[1]{0:T(128)S(6)} %copy.11.stiffness_ref, f32[3]{0:T(128)S(1)} %copy-done.4, f32[3,64,512]{2,1,0:T(8,128)S(1)} %copy-done, f32[3,64,512]{2,1,0:T(8,128)S(1)} %collective-permute-done.below_ref, ...), custom_call_target="tpu_custom_call" | custom-call | flops 20971520 | bytes 2097152 | tf_op jit(solution)/shard_map/exchange/pallas_call | solution.py:573
  22.6 9.4 %all-to-all-done.rows_ref = f32[32,16,384]{2,1,0:T(8,128)S(1)} async-done(((f32[32,16,384]{2,1,0:T(8,128)}), f32[32,16,384]{2,1,0:T(8,128)S(1)}, u32[]{:S(2)}, u32[]{:S(2)}) %all-to-all-start) | async-done | bytes 786464 | tf_op jit(solution)/shard_map/all_to_all | solution.py:586
  32.0 3.3 %middle.1 = f32[32,16,384]{2,1,0:T(8,128)S(1)} custom-call(f32[32,16,384]{2,1,0:T(8,128)S(1)} %all-to-all-done.rows_ref, f32[6,8,16,128]{3,2,1,0:T(8,128)S(1)} %get-tuple-element.23.coef_ref, f32[6,8,128]{2,1,0:T(8,128)S(1)} %get-tuple-element.24.edge_ref, f32[16,128]{1,0:T(8,128)S(1)} %get-tuple-element.25.sign_ref, ...), custom_call_target="tpu_custom_call" | custom-call | flops 2097152000 | bytes 4194304 | tf_op jit(solution)/shard_map/middle/pallas_call | solution.py:588
  35.3 0.0 copy-start.5
  35.3 0.0 collective-permute-done.2.before_any
  35.3 0.0 collective-permute-done.3.after_any
  35.3 23.9 %all_to_all.10 = f32[32,16,384]{2,1,0:T(8,128)S(1)} all-to-all(f32[32,16,384]{2,1,0:T(8,128)S(1)} %middle.1), channel_id=1, replica_groups=mesh['layer'=4,'plane'=8] {'plane','layer'}, dimensions={0} | all-to-all | bytes 1572864 | tf_op jit(solution)/shard_map/all_to_all | solution.py:599
  59.2 0.0 copy-done.5
  59.2 1.8 %last.1 = (f32[3,64,512]{2,1,0:T(8,128)}, f32[3,64,512]{2,1,0:T(8,128)}) custom-call(f32[8,512]{1,0:T(8,128)S(1)} %collective-permute-done.2.before_any, f32[8,512]{1,0:T(8,128)S(1)} %collective-permute-done.3.after_any, f32[8,512]{1,0:T(8,128)S(1)} %get-tuple-element.31.scale_any, f32[3,64,512]{2,1,0:T(8,128)S(1)} %copy-done, ...), custom_call_target="tpu_custom_call" | custom-call | flops 1207959552 | bytes 4194304 | tf_op jit(solution)/shard_map/last/pallas_call | solution.py:601
  (1 shorter events, 0.0 us)
Async XLA Ops:
  3.9 7.4 %copy-start = (f32[3,64,512]{2,1,0:T(8,128)S(1)}, f32[3,64,512]{2,1,0:T(8,128)}, u32[]{:S(2)}) copy-start(f32[3,64,512]{2,1,0:T(8,128)} %get-tuple-element.20.moment_ref) | copy-start | bytes 1179652
  3.9 10.9 %copy-start.6 = (f32[2,8,512]{2,1,0:T(8,128)S(1)}, f32[2,8,512]{2,1,0:T(8,128)}, u32[]{:S(2)}) copy-start(f32[2,8,512]{2,1,0:T(8,128)} %get-tuple-element.28) | copy-start | bytes 98308
  3.9 16.5 %copy-start.1 = (bf16[2,256,256]{2,1,0:T(8,128)(2,1)S(1)}, bf16[2,256,256]{2,1,0:T(8,128)(2,1)}, u32[]{:S(2)}) copy-start(bf16[2,256,256]{2,1,0:T(8,128)(2,1)} %constant.17.clone.back_hbm.refs_1_.back_ref) | copy-start | bytes 786436
  3.9 28.1 %all-to-all-start = ((f32[32,16,384]{2,1,0:T(8,128)}), f32[32,16,384]{2,1,0:T(8,128)S(1)}, u32[]{:S(2)}, u32[]{:S(2)}) async-start(f32[32,16,384]{2,1,0:T(8,128)} %bitcast.16), calls=%async_computation | async-start | bytes 1572864 | tf_op jit(solution)/shard_map/all_to_all | solution.py:586
  11.2 9.1 %copy-start.3 = (f32[2,8,8,128]{3,2,1,0:T(8,128)S(1)}, f32[2,8,8,128]{3,2,1,0:T(8,128)}, u32[]{:S(2)}) copy-start(f32[2,8,8,128]{3,2,1,0:T(8,128)} %constant.18.clone.twiddle_hbm.refs_0_.twiddle_ref) | copy-start | bytes 196612
  11.3 9.8 %collective-permute-start = (f32[3,64,512]{2,1,0:T(8,128)S(1)}, f32[3,64,512]{2,1,0:T(8,128)S(1)}, u32[]{:S(2)}, u32[]{:S(2)}) collective-permute-start(f32[3,64,512]{2,1,0:T(8,128)S(1)} %copy-done), channel_id=1, source_target_pairs={{0,8},{8,16},{16,24},{1,9},{9,17},{17,25},{2,10},{10,18},{18,26},{... | collective-permute-start | bytes 1179656 | tf_op jit(solution)/shard_map/ppermute | solution.py:509
  13.5 7.7 %collective-permute-start.1 = (f32[3,64,512]{2,1,0:T(8,128)S(1)}, f32[3,64,512]{2,1,0:T(8,128)S(1)}, u32[]{:S(2)}, u32[]{:S(2)}) collective-permute-start(f32[3,64,512]{2,1,0:T(8,128)S(1)} %copy-done), channel_id=1, source_target_pairs={{8,0},{16,8},{24,16},{9,1},{17,9},{25,17},{10,2},{18,10},{26,18},{... | collective-permute-start | bytes 1179656 | tf_op jit(solution)/shard_map/ppermute | solution.py:509
  14.8 20.5 %collective-permute-start.2 = (f32[8,512]{1,0:T(8,128)S(1)}, f32[8,512]{1,0:T(8,128)S(1)}, u32[]{:S(2)}, u32[]{:S(2)}) collective-permute-start(f32[8,512]{1,0:T(8,128)S(1)} %get-tuple-element.37), channel_id=1, source_target_pairs={{0,1},{1,2},{2,3},{3,4},{4,5},{5,6},{6,7},{8,9},{9,10},{10,11},{11... | collective-permute-start | bytes 49160 | tf_op jit(solution)/shard_map/ppermute | solution.py:509
  18.3 17.0 %collective-permute-start.3 = (f32[8,512]{1,0:T(8,128)S(1)}, f32[8,512]{1,0:T(8,128)S(1)}, u32[]{:S(2)}, u32[]{:S(2)}) collective-permute-start(f32[8,512]{1,0:T(8,128)S(1)} %get-tuple-element.36), channel_id=1, source_target_pairs={{1,0},{2,1},{3,2},{4,3},{5,4},{6,5},{7,6},{9,8},{10,9},{11,10},{12... | collective-permute-start | bytes 49160 | tf_op jit(solution)/shard_map/ppermute | solution.py:509
  20.4 0.9 %copy-start.2 = (f32[1,64,512]{2,1,0:T(8,128)S(1)}, f32[1,64,512]{2,1,0:T(8,128)}, u32[]{:S(2)}) copy-start(f32[1,64,512]{2,1,0:T(8,128)} %param.12) | copy-start | bytes 393220
  21.1 0.7 %copy-start.4 = (f32[3]{0:T(128)S(1)}, f32[3]{0:T(128)}, u32[]{:S(2)}) copy-start(f32[3]{0:T(128)} %coupling_ref.1) | copy-start | bytes 40
  35.3 23.9 %copy-start.5 = (bf16[2,256,256]{2,1,0:T(8,128)(2,1)S(1)}, bf16[2,256,256]{2,1,0:T(8,128)(2,1)}, u32[]{:S(2)}) copy-start(bf16[2,256,256]{2,1,0:T(8,128)(2,1)} %constant.16.clone.edge_hbm.edge_ref) | copy-start | bytes 786436

commit v4 on v3

--- a/solution.py
+++ b/solution.py
@@ -95,7 +95,7 @@
     ]
     for copy in loads:
         copy.start()
-    for copy in loads:
+    for copy in loads[:3]:
         copy.wait()
     sin_polar, cos_polar = sine_cosine(angle_ref[0])
     sin_half, cos_half = sine_cosine(0.5 * angle_ref[1])
@@ -105,6 +105,8 @@
         sin_polar * (2.0 * sin_half * cos_half),
         cos_polar,
     )
+    for copy in loads[3:]:
+        copy.wait()
     groups = [[] for _ in range(4)]
     for c in range(3):
         moment_ref[c] = moment[c]
@@ -348,8 +350,8 @@
     lower = [jnp.concatenate([b[:lanes, lanes:], b[lanes:, lanes:]], axis=1) for b in back]
     forward = tuple(jnp.concatenate(pair) for pair in zip(upper, lower))
 
-    def run(step, carry):
-        here = pl.ds(pl.multiple_of(step * sublanes, sublanes), sublanes)
+    def run(step):
+        here = slice(step * sublanes, (step + 1) * sublanes)
 
         def piece(row, part):
             tile, upper = divmod(part, 2)
@@ -368,31 +370,31 @@
                     cosine, sine = twiddle_ref[0, r], twiddle_ref[1, r]
                     real, imag = real * cosine + imag * sine, imag * cosine - real * sine
                 start = item * sublanes
-                work_ref[r, start : start + sublanes, :lanes] = real
-                work_ref[r, start : start + sublanes, lanes:] = imag
+                work_ref[step, r, start : start + sublanes, :lanes] = real
+                work_ref[step, r, start : start + sublanes, lanes:] = imag
         for r in range(radix):
-            work_ref[r] = product(split(work_ref[r]), forward, dims)
+            work_ref[step, r] = product(split(work_ref[step, r]), forward, dims)
         for r in range(radix):
-            value = work_ref[r]
+            value = work_ref[step, r]
             cuts = [slice(item * sublanes, (item + 1) * sublanes) for item in range(items)]
             pairs = [(value[cut, :lanes], value[cut, lanes:]) for cut in cuts]
             spectrum = [pairs[3 * t : 3 * t + 3] for t in range(layers)]
             coef = [coef_ref[n, r, here] for n in range(coef_count)]
             coef += [edge_ref[n, r : r + 1] for n in range(coef_count)] + [sign_ref[here]]
             out = respond(spectrum, coef, r == 0, place * radix + r == radix * half)
-            work_ref[r] = jnp.concatenate(
+            work_ref[step, r] = jnp.concatenate(
                 [jnp.concatenate([pair[0], pair[1]], axis=1) for layer in out for pair in layer]
             )
         for r in range(radix):
-            work_ref[r] = product(split(work_ref[r]), back, dims)
+            work_ref[step, r] = product(split(work_ref[step, r]), back, dims)
         for layer in range(layers):
             parts = [[None] * 6 for _ in range(pieces)]
             for c in range(3):
                 start = (layer * 3 + c) * sublanes
                 v = []
                 for r in range(radix):
-                    real = work_ref[r, start : start + sublanes, :lanes]
-                    imag = work_ref[r, start : start + sublanes, lanes:]
+                    real = work_ref[step, r, start : start + sublanes, :lanes]
+                    imag = work_ref[step, r, start : start + sublanes, lanes:]
                     if r > 0:
                         cosine, sine = twiddle_ref[0, r], twiddle_ref[1, r]
                         real, imag = real * cosine - imag * sine, imag * cosine + real * sine
@@ -406,9 +408,9 @@
                     cut = slice(tile * lanes, (tile + 1) * lanes)
                     out_ref[row, here, cut] = jnp.where(low, first, pltpu.roll(second, half, 1))
                     out_ref[row + layers, here, cut] = jnp.where(low, pltpu.roll(first, half, 1), second)
-        return carry
-
-    lax.fori_loop(0, steps, run, 0)
+
+    for step in range(steps):
+        run(step)
 
 
 def exchange_kernel(place_ref, stiffness_ref, coupling_ref, moment_ref, below_ref, above_ref, anisotropy_ref, out_ref, scale_ref):
@@ -590,7 +592,7 @@
         out_shape=jax.ShapeDtypeStruct((device_count, slots, width), f32),
         in_specs=[in_vmem] * 6,
         out_specs=in_vmem,
-        scratch_shapes=[pltpu.VMEM((radix, layers * 3 * sublanes, 2 * lanes), f32)],
+        scratch_shapes=[pltpu.VMEM((slots // sublanes, radix, layers * 3 * sublanes, 2 * lanes), f32)],
         compiler_params=small,
         cost_estimate=pl.CostEstimate(flops=2000 << 20, bytes_accessed=4 << 20, transcendentals=0),
         name="middle",

time: 61.3 us -> 60.9 us (level)
  no operation moved by 1% of the time
where the time goes in v4:
time: 60.9 us; the launch traced here: 60.5 us
  blocking collectives  23.9 us (39%)
  starting transfers between devices  15.6 us (26%)
  Pallas kernels  9.43 us (15%)
  waiting for transfers between devices  9.37 us (15%)
  between operations  1.46 us (2%)
  local copies, waits for them, and re-layouts  0.68 us (1%)
    all_to_all x1, blocking collectives, fast_body(): block = exchange_all(block)  23.9 us
    all_to_all x1, waiting for transfers between devices, fast_body(): block = exchange_all(block.reshape(device_count, slots, width))  9.36 us
    ppermute x4, starting transfers between devices, shift(): return lax.ppermute(value, axis, pairs)  8.3 us
    all_to_all x1, starting transfers between devices, fast_body(): block = exchange_all(block.reshape(device_count, slots, width))  7.33 us
    pallas_call x1, Pallas kernels, fast_body(): pl.pallas_call(first_kernel, out_shape=[field_shape, jax.ShapeDtypeStruct...  3.11 us
    pallas_call x1, Pallas kernels, fast_body(): pl.pallas_call(functools.partial(middle_kernel, layers=layers), out_shape...  2.95 us
    pallas_call x1, Pallas kernels, fast_body(): pl.pallas_call(last_kernel, out_shape=[field_shape] * 2, in_specs=[in_any...  1.77 us
  transfers between devices with their start and end apart: 5, of which 1 were waited for; matrix products, arithmetic and copies ran while one was open for 0% of the time, Pallas kernels for 8%

profile of v4, /device:TPU:0, one launch (start us, length us, event | category | flops | bytes accessed | tf_op | source)
XLA Modules:
  0.0 60.5 jit_solution(16232205861944158482)
XLA Ops:
  0.6 3.1 %first.1 = (f32[3,64,512]{2,1,0:T(8,128)}, f32[2,8,512]{2,1,0:T(8,128)}, f32[512,384]{1,0:T(8,128)}) custom-call(f32[64,512]{1,0:T(8,128)} %bitcast.17, f32[64,512]{1,0:T(8,128)} %bitcast.18, f32[64,512]{1,0:T(8,128)} %bitcast.19, bf16[2,256,256]{2,1,0:T(8,128)(2,1)} %constant.16.clone.edge_hbm.edge_ref, ...), custom_call_target="tpu_custom_call" | custom-call | flops 1207959552 | bytes 4194304 | tf_op jit(solution)/shard_map/first/pallas_call | solution.py:534
  3.7 0.0 copy-start
  3.8 0.0 copy-start.6
  3.8 0.0 copy-start.1
  3.8 7.3 %all-to-all-start = ((f32[32,16,384]{2,1,0:T(8,128)}), f32[32,16,384]{2,1,0:T(8,128)S(1)}, u32[]{:S(2)}, u32[]{:S(2)}) async-start(f32[32,16,384]{2,1,0:T(8,128)} %bitcast.16), calls=%async_computation | async-start | bytes 1572864 | tf_op jit(solution)/shard_map/all_to_all | solution.py:588
  11.1 0.0 copy-start.3
  11.1 0.0 copy-done
  11.1 2.2 %collective-permute-start = (f32[3,64,512]{2,1,0:T(8,128)S(1)}, f32[3,64,512]{2,1,0:T(8,128)S(1)}, u32[]{:S(2)}, u32[]{:S(2)}) collective-permute-start(f32[3,64,512]{2,1,0:T(8,128)S(1)} %copy-done), channel_id=1, source_target_pairs={{0,8},{8,16},{16,24},{1,9},{9,17},{17,25},{2,10},{10,18},{18,26},{... | collective-permute-start | bytes 1179656 | tf_op jit(solution)/shard_map/ppermute | solution.py:511
  13.3 1.3 %collective-permute-start.1 = (f32[3,64,512]{2,1,0:T(8,128)S(1)}, f32[3,64,512]{2,1,0:T(8,128)S(1)}, u32[]{:S(2)}, u32[]{:S(2)}) collective-permute-start(f32[3,64,512]{2,1,0:T(8,128)S(1)} %copy-done), channel_id=1, source_target_pairs={{8,0},{16,8},{24,16},{9,1},{17,9},{25,17},{10,2},{18,10},{26,18},{... | collective-permute-start | bytes 1179656 | tf_op jit(solution)/shard_map/ppermute | solution.py:511
  14.6 0.0 copy-done.6
  14.7 3.5 %collective-permute-start.2 = (f32[8,512]{1,0:T(8,128)S(1)}, f32[8,512]{1,0:T(8,128)S(1)}, u32[]{:S(2)}, u32[]{:S(2)}) collective-permute-start(f32[8,512]{1,0:T(8,128)S(1)} %get-tuple-element.37), channel_id=1, source_target_pairs={{0,1},{1,2},{2,3},{3,4},{4,5},{5,6},{6,7},{8,9},{9,10},{10,11},{11... | collective-permute-start | bytes 49160 | tf_op jit(solution)/shard_map/ppermute | solution.py:511
  18.2 1.3 %collective-permute-start.3 = (f32[8,512]{1,0:T(8,128)S(1)}, f32[8,512]{1,0:T(8,128)S(1)}, u32[]{:S(2)}, u32[]{:S(2)}) collective-permute-start(f32[8,512]{1,0:T(8,128)S(1)} %get-tuple-element.36), channel_id=1, source_target_pairs={{1,0},{2,1},{3,2},{4,3},{5,4},{6,5},{7,6},{9,8},{10,9},{11,10},{12... | collective-permute-start | bytes 49160 | tf_op jit(solution)/shard_map/ppermute | solution.py:511
  20.2 0.1 pad_add_fusion.place_ref.base_ref
  20.2 0.0 copy-done.1
  20.2 0.0 copy-done.3
  20.2 0.0 copy-start.2
  20.2 0.7 %coefs.1 = (f32[6,8,16,128]{3,2,1,0:T(8,128)S(1)}, f32[6,8,128]{2,1,0:T(8,128)S(1)}, f32[16,128]{1,0:T(8,128)S(1)}, f32[2,8,8,128]{3,2,1,0:T(8,128)S(1)}, bf16[2,256,256]{2,1,0:T(8,128)(2,1)S(1)}) custom-call(s32[2]{0:T(128)S(1)} %pad_add_fusion.place_ref.base_ref, f32[2,8,8,128]{3,2,1,0:T(8,128)S(1)} %copy-done.3, bf16[2,256,256]{2,1,0:T(8,128)(2,1)S(1)} %copy-done.1), custom_call_target="tpu_custom_call" | custom-call | flops 20971520 | bytes 1048576 | tf_op jit(solution)/shard_map/coefs/pallas_call | solution.py:556
  21.0 0.0 copy-start.4
  21.0 0.0 collective-permute-done.below_ref
  21.0 0.0 collective-permute-done.1.above_ref
  21.0 0.1 copy-done.2
  21.1 0.5 copy-done.4
  21.6 0.9 %exchange.1 = (f32[3,64,512]{2,1,0:T(8,128)S(1)}, f32[8,512]{1,0:T(8,128)S(1)}) custom-call(s32[2]{0:T(128)S(1)} %pad_add_fusion.place_ref.base_ref, f32[1]{0:T(128)S(6)} %copy.11.stiffness_ref, f32[3]{0:T(128)S(1)} %copy-done.4, f32[3,64,512]{2,1,0:T(8,128)S(1)} %copy-done, f32[3,64,512]{2,1,0:T(8,128)S(1)} %collective-permute-done.below_ref, ...), custom_call_target="tpu_custom_call" | custom-call | flops 20971520 | bytes 2097152 | tf_op jit(solution)/shard_map/exchange/pallas_call | solution.py:575
  22.5 9.4 %all-to-all-done.rows_ref = f32[32,16,384]{2,1,0:T(8,128)S(1)} async-done(((f32[32,16,384]{2,1,0:T(8,128)}), f32[32,16,384]{2,1,0:T(8,128)S(1)}, u32[]{:S(2)}, u32[]{:S(2)}) %all-to-all-start) | async-done | bytes 786464 | tf_op jit(solution)/shard_map/all_to_all | solution.py:588
  31.9 2.9 %middle.1 = f32[32,16,384]{2,1,0:T(8,128)S(1)} custom-call(f32[32,16,384]{2,1,0:T(8,128)S(1)} %all-to-all-done.rows_ref, f32[6,8,16,128]{3,2,1,0:T(8,128)S(1)} %get-tuple-element.23.coef_ref, f32[6,8,128]{2,1,0:T(8,128)S(1)} %get-tuple-element.24.edge_ref, f32[16,128]{1,0:T(8,128)S(1)} %get-tuple-element.25.sign_ref, ...), custom_call_target="tpu_custom_call" | custom-call | flops 2097152000 | bytes 4194304 | tf_op jit(solution)/shard_map/middle/pallas_call | solution.py:590
  34.8 0.0 copy-start.5
  34.9 0.0 collective-permute-done.2.before_any
  34.9 0.0 collective-permute-done.3.after_any
  34.9 23.9 %all_to_all.10 = f32[32,16,384]{2,1,0:T(8,128)S(1)} all-to-all(f32[32,16,384]{2,1,0:T(8,128)S(1)} %middle.1), channel_id=1, replica_groups=mesh['layer'=4,'plane'=8] {'plane','layer'}, dimensions={0} | all-to-all | bytes 1572864 | tf_op jit(solution)/shard_map/all_to_all | solution.py:601
  58.8 0.0 copy-done.5
  58.8 1.8 %last.1 = (f32[3,64,512]{2,1,0:T(8,128)}, f32[3,64,512]{2,1,0:T(8,128)}) custom-call(f32[8,512]{1,0:T(8,128)S(1)} %collective-permute-done.2.before_any, f32[8,512]{1,0:T(8,128)S(1)} %collective-permute-done.3.after_any, f32[8,512]{1,0:T(8,128)S(1)} %get-tuple-element.31.scale_any, f32[3,64,512]{2,1,0:T(8,128)S(1)} %copy-done, ...), custom_call_target="tpu_custom_call" | custom-call | flops 1207959552 | bytes 4194304 | tf_op jit(solution)/shard_map/last/pallas_call | solution.py:603
  (1 shorter events, 0.0 us)
Async XLA Ops:
  3.7 7.4 %copy-start = (f32[3,64,512]{2,1,0:T(8,128)S(1)}, f32[3,64,512]{2,1,0:T(8,128)}, u32[]{:S(2)}) copy-start(f32[3,64,512]{2,1,0:T(8,128)} %get-tuple-element.20.moment_ref) | copy-start | bytes 1179652
  3.8 10.9 %copy-start.6 = (f32[2,8,512]{2,1,0:T(8,128)S(1)}, f32[2,8,512]{2,1,0:T(8,128)}, u32[]{:S(2)}) copy-start(f32[2,8,512]{2,1,0:T(8,128)} %get-tuple-element.28) | copy-start | bytes 98308
  3.8 16.5 %copy-start.1 = (bf16[2,256,256]{2,1,0:T(8,128)(2,1)S(1)}, bf16[2,256,256]{2,1,0:T(8,128)(2,1)}, u32[]{:S(2)}) copy-start(bf16[2,256,256]{2,1,0:T(8,128)(2,1)} %constant.17.clone.back_hbm.refs_1_.back_ref) | copy-start | bytes 786436
  3.8 28.1 %all-to-all-start = ((f32[32,16,384]{2,1,0:T(8,128)}), f32[32,16,384]{2,1,0:T(8,128)S(1)}, u32[]{:S(2)}, u32[]{:S(2)}) async-start(f32[32,16,384]{2,1,0:T(8,128)} %bitcast.16), calls=%async_computation | async-start | bytes 1572864 | tf_op jit(solution)/shard_map/all_to_all | solution.py:588
  11.1 9.1 %copy-start.3 = (f32[2,8,8,128]{3,2,1,0:T(8,128)S(1)}, f32[2,8,8,128]{3,2,1,0:T(8,128)}, u32[]{:S(2)}) copy-start(f32[2,8,8,128]{3,2,1,0:T(8,128)} %constant.18.clone.twiddle_hbm.refs_0_.twiddle_ref) | copy-start | bytes 196612
  11.1 9.8 %collective-permute-start = (f32[3,64,512]{2,1,0:T(8,128)S(1)}, f32[3,64,512]{2,1,0:T(8,128)S(1)}, u32[]{:S(2)}, u32[]{:S(2)}) collective-permute-start(f32[3,64,512]{2,1,0:T(8,128)S(1)} %copy-done), channel_id=1, source_target_pairs={{0,8},{8,16},{16,24},{1,9},{9,17},{17,25},{2,10},{10,18},{18,26},{... | collective-permute-start | bytes 1179656 | tf_op jit(solution)/shard_map/ppermute | solution.py:511
  13.3 7.7 %collective-permute-start.1 = (f32[3,64,512]{2,1,0:T(8,128)S(1)}, f32[3,64,512]{2,1,0:T(8,128)S(1)}, u32[]{:S(2)}, u32[]{:S(2)}) collective-permute-start(f32[3,64,512]{2,1,0:T(8,128)S(1)} %copy-done), channel_id=1, source_target_pairs={{8,0},{16,8},{24,16},{9,1},{17,9},{25,17},{10,2},{18,10},{26,18},{... | collective-permute-start | bytes 1179656 | tf_op jit(solution)/shard_map/ppermute | solution.py:511
  14.7 20.2 %collective-permute-start.2 = (f32[8,512]{1,0:T(8,128)S(1)}, f32[8,512]{1,0:T(8,128)S(1)}, u32[]{:S(2)}, u32[]{:S(2)}) collective-permute-start(f32[8,512]{1,0:T(8,128)S(1)} %get-tuple-element.37), channel_id=1, source_target_pairs={{0,1},{1,2},{2,3},{3,4},{4,5},{5,6},{6,7},{8,9},{9,10},{10,11},{11... | collective-permute-start | bytes 49160 | tf_op jit(solution)/shard_map/ppermute | solution.py:511
  18.2 16.7 %collective-permute-start.3 = (f32[8,512]{1,0:T(8,128)S(1)}, f32[8,512]{1,0:T(8,128)S(1)}, u32[]{:S(2)}, u32[]{:S(2)}) collective-permute-start(f32[8,512]{1,0:T(8,128)S(1)} %get-tuple-element.36), channel_id=1, source_target_pairs={{1,0},{2,1},{3,2},{4,3},{5,4},{6,5},{7,6},{9,8},{10,9},{11,10},{12... | collective-permute-start | bytes 49160 | tf_op jit(solution)/shard_map/ppermute | solution.py:511
  20.2 0.9 %copy-start.2 = (f32[1,64,512]{2,1,0:T(8,128)S(1)}, f32[1,64,512]{2,1,0:T(8,128)}, u32[]{:S(2)}) copy-start(f32[1,64,512]{2,1,0:T(8,128)} %param.12) | copy-start | bytes 393220
  21.0 0.7 %copy-start.4 = (f32[3]{0:T(128)S(1)}, f32[3]{0:T(128)}, u32[]{:S(2)}) copy-start(f32[3]{0:T(128)} %coupling_ref.1) | copy-start | bytes 40
  34.8 23.9 %copy-start.5 = (bf16[2,256,256]{2,1,0:T(8,128)(2,1)S(1)}, bf16[2,256,256]{2,1,0:T(8,128)(2,1)}, u32[]{:S(2)}) copy-start(bf16[2,256,256]{2,1,0:T(8,128)(2,1)} %constant.16.clone.edge_hbm.edge_ref) | copy-start | bytes 786436
